TPU v7x, 8 devices: a whole 2x2x1 slice. The times are simulated.
8 devices in a mesh: dp: 1 (over z), col: 2 (over y), row: 4 (over x, core).
Axes of the slice: x: 2, y: 2, z: 1, core: 2. Of those that a mesh axis runs over, the one named last changes fastest.
Arguments:
- x_act: bfloat16 [96, 5120], P(('dp', 'row'), 'col')
- ln_gain: float32 [5120], P('col')
- w_in: bfloat16 [5120, 20480], P('row', 'col')
- w_out: bfloat16 [20480, 5120], P('row', 'col')
Outputs:
- output: bfloat16 [96, 5120], P(('dp', 'row'), 'col')
All inputs are finite; a program needn't handle non-finite values.
Results may differ from a plain program's by a relative error of at most 0.00117.
Values are sent between devices in bfloat16 or wider.
A program may use at most 1 GiB of HBM per device.

v0:
```python
import jax
import jax.numpy as jnp
from jax import lax
from jax.sharding import PartitionSpec as P

NORM_EPS = 1e-5


def solution(mesh):
    col_size = mesh.shape["col"]

    def local_block(x_blk, gain_blk, w_in_blk, w_out_blk):
        d_model = x_blk.shape[1] * col_size
        x_f32 = x_blk.astype(jnp.float32)
        part_stats = jnp.stack([jnp.sum(x_f32, axis=1), jnp.sum(x_f32 * x_f32, axis=1)])
        row_stats = lax.psum(part_stats, "col") / d_model
        row_mean = row_stats[0][:, None]
        row_var = row_stats[1][:, None] - row_mean * row_mean
        z_blk = ((x_f32 - row_mean) * lax.rsqrt(row_var + NORM_EPS) * gain_blk).astype(jnp.bfloat16)
        z_rows = lax.all_gather(z_blk, "col", axis=1, tiled=True)
        z_cols = lax.all_to_all(z_rows, "row", 1, 0, tiled=True)
        up_part = jnp.dot(z_cols, w_in_blk, preferred_element_type=jnp.float32)
        up_sum = lax.psum_scatter(up_part, "row", scatter_dimension=0, tiled=True)
        h_blk = jax.nn.gelu(up_sum, approximate=True).astype(jnp.bfloat16)
        h_rows = lax.all_gather(h_blk, "col", axis=1, tiled=True)
        h_cols = lax.all_to_all(h_rows, "row", 1, 0, tiled=True)
        down_part = jnp.dot(h_cols, w_out_blk, preferred_element_type=jnp.float32)
        down_sum = lax.psum_scatter(down_part, "row", scatter_dimension=0, tiled=True)
        return (x_f32 + down_sum).astype(jnp.bfloat16)

    return jax.shard_map(
        local_block,
        mesh=mesh,
        in_specs=(P(("dp", "row"), "col"), P("col"), P("row", "col"), P("row", "col")),
        out_specs=P(("dp", "row"), "col"),
        check_vma=False,
    )
```

profile of v0, /device:TPU:0, one launch (start us, length us, event | category | flops | bytes accessed | tf_op | source)
XLA Modules:
  0.0 151.0 jit_solution(15759563347296206176)
XLA Ops:
  6.5 0.0 reduce-scatter.7.cloned.1.call-start
  6.5 1.0 convert_reduce_fusion
  7.6 6.3 %psum.7 = f32[2,24]{1,0:T(2,128)S(1)} all-reduce(f32[2,24]{1,0:T(2,128)S(1)} %pad_maximum_fusion), channel_id=1, replica_groups=mesh['dp'=1,'col'=2,'row'=4] {'col'}, use_global_device_ids=true, to_apply=%region_2.0 | all-reduce | flops 48 | bytes 384 | tf_op jit(solution)/shard_map/psum | solution.py:16
  13.9 1.0 fusion.11
  14.9 5.6 %all_gather.6 = bf16[24,5120]{1,0:T(8,128)(2,1)S(1)} all-gather(bf16[24,2560]{1,0:T(8,128)(2,1)S(1)} %fusion.11), channel_id=1, replica_groups=mesh['dp'=1,'col'=2,'row'=4] {'col'}, dimensions={1}, use_global_device_ids=true | all-gather | bytes 368640 | tf_op jit(solution)/shard_map/all_gather | solution.py:20
  20.5 8.9 %all_to_all.38 = bf16[24,4,1280]{2,0,1:T(8,128)(2,1)S(1)} all-to-all(bf16[24,4,1280]{2,0,1:T(8,128)(2,1)S(1)} %bitcast.35), channel_id=1, replica_groups=mesh['dp'=1,'col'=2,'row'=4] {'row'}, dimensions={1} | all-to-all | bytes 491520 | tf_op jit(solution)/shard_map/all_to_all | solution.py:21
  29.4 14.6 %fusion.15 = f32[96,10240]{1,0:T(8,128)} fusion(bf16[96,1280]{1,0:T(8,128)(2,1)S(1)} %bitcast.36, bf16[1280,10240]{1,0:T(8,128)(2,1)} %param.6), kind=kOutput, calls=%fused_computation.26 | convolution fusion | flops 2516582400 | bytes 30392320 | tf_op jit(solution)/shard_map/dot_general | solution.py:22
  43.9 0.0 copy-start
  43.9 0.0 reduce-scatter.7.cloned.1.call-update
  44.0 0.0 reduce-scatter.9.cloned.1.call-start
  44.0 36.9 %reduce-scatter.7.cloned.1.call-done = f32[24,10240]{1,0:T(8,128)} async-done(((f32[96,10240]{1,0:T(8,128)}), f32[24,10240]{1,0:T(8,128)}) %reduce-scatter.7.cloned.1.call-update) | async-done | bytes 983056
  80.9 1.5 %fusion.7 = bf16[24,10240]{1,0:T(8,128)(2,1)S(1)} fusion(f32[24,10240]{1,0:T(8,128)} %reduce-scatter.7.cloned.1.call-done), kind=kLoop, calls=%fused_computation.8 | loop fusion | flops 2211840 | bytes 1474560 | tf_op jit(solution)/shard_map/convert_element_type | solution.py:24
  82.4 13.4 %all_gather.7 = bf16[24,20480]{1,0:T(8,128)(2,1)S(1)} all-gather(bf16[24,10240]{1,0:T(8,128)(2,1)S(1)} %fusion.7), channel_id=1, replica_groups=mesh['dp'=1,'col'=2,'row'=4] {'col'}, dimensions={1}, use_global_device_ids=true | all-gather | bytes 1474560 | tf_op jit(solution)/shard_map/all_gather | solution.py:25
  95.8 0.1 copy.15
  95.8 16.1 %all_to_all.39 = bf16[24,4,5120]{2,0,1:T(8,128)(2,1)S(1)} all-to-all(bf16[24,4,5120]{2,0,1:T(8,128)(2,1)S(1)} %bitcast.33), channel_id=1, replica_groups=mesh['dp'=1,'col'=2,'row'=4] {'row'}, dimensions={1} | all-to-all | bytes 1966080 | tf_op jit(solution)/shard_map/all_to_all | solution.py:26
  112.0 11.6 %fusion.16 = f32[96,2560]{1,0:T(8,128)} fusion(bf16[96,5120]{1,0:T(8,128)(2,1)S(1)} %bitcast.31, bf16[5120,2560]{1,0:T(8,128)(2,1)} %param.7), kind=kOutput, calls=%fused_computation.27 | convolution fusion | flops 2516582400 | bytes 28180480 | tf_op jit(solution)/shard_map/dot_general | solution.py:27
  123.6 0.0 reduce-scatter.9.cloned.1.call-update
  123.6 18.9 %reduce-scatter.9.cloned.1.call-done = f32[24,2560]{1,0:T(8,128)} async-done(((f32[96,2560]{1,0:T(8,128)}), f32[24,2560]{1,0:T(8,128)}) %reduce-scatter.9.cloned.1.call-update) | async-done | bytes 245776
  142.5 0.0 copy-done
  142.5 1.6 %fusion.12 = bf16[24,2560]{1,0:T(8,128)(2,1)} fusion(f32[24,2560]{1,0:T(8,128)} %reduce-scatter.9.cloned.1.call-done, bf16[24,2560]{1,0:T(8,128)(2,1)S(1)} %copy-done), kind=kLoop, calls=%fused_computation.18 | loop fusion | flops 184320 | bytes 491520 | tf_op jit(solution)/shard_map/convert_element_type | solution.py:29
  (5 shorter events, 0.0 us)
Async XLA Ops:
  6.5 74.4 %reduce-scatter.7.cloned.1.call-start = ((), (), s32[]{:S(2)}) async-start(), calls=%async_computation.4 | async-start | bytes 4915200
  43.9 98.6 %copy-start = (bf16[24,2560]{1,0:T(8,128)(2,1)S(1)}, bf16[24,2560]{1,0:T(8,128)(2,1)}, u32[]{:S(2)}) copy-start(bf16[24,2560]{1,0:T(8,128)(2,1)} %param.4) | copy-start | bytes 368644
  44.0 98.5 %reduce-scatter.9.cloned.1.call-start = ((), (), s32[]{:S(2)}) async-start(), calls=%async_computation.5 | async-start | bytes 1228800
Sparse Core Ops, SparseCore 0:
  44.1 36.7 reduce-scatter.6
  123.7 18.7 reduce-scatter.8
where the time goes:
time: 151 us
  waiting for transfers between devices  55.8 us (37%)
  blocking collectives  50.2 us (33%)
  matrix products  26.2 us (17%)
  between operations  13.4 us (9%)
  other arithmetic  5.21 us (3%)
    unnamed x4, waiting for transfers between devices  55.8 us
    all_to_all x1, blocking collectives, local_block(): h_cols = lax.all_to_all(h_rows, 'row', 1, 0, tiled=True)  16.1 us
    dot_general x1, matrix products, local_block(): up_part = jnp.dot(z_cols, w_in_blk, preferred_element_type=jnp.float32)  14.6 us
    all_gather x1, blocking collectives, local_block(): h_rows = lax.all_gather(h_blk, 'col', axis=1, tiled=True)  13.4 us
    dot_general x1, matrix products, local_block(): down_part = jnp.dot(h_cols, w_out_blk, preferred_element_type=jnp.float32)  11.6 us
    all_to_all x1, blocking collectives, local_block(): z_cols = lax.all_to_all(z_rows, 'row', 1, 0, tiled=True)  8.89 us
    psum x1, blocking collectives, local_block(): row_stats = lax.psum(part_stats, 'col') / d_model  6.27 us
    all_gather x1, blocking collectives, local_block(): z_rows = lax.all_gather(z_blk, 'col', axis=1, tiled=True)  5.56 us
  transfers between devices with their start and end apart: 2, of which 2 were waited for; matrix products, arithmetic and copies ran while one was open for 0% of the time, Pallas kernels for 0%

commit v1 on v0

v1 whole, which is shorter than its diff:
```python
import jax
import jax.numpy as jnp
from jax import lax
from jax.experimental import pallas as pl
from jax.experimental.pallas import tpu as pltpu
from jax.sharding import PartitionSpec as P

NORM_EPS = 1e-5
MESH = pl.DeviceIdType.MESH
F32 = jnp.float32
BF16 = jnp.bfloat16

C = 256
NA = 12
NB = 8
N = NA + NB
TAIL = 5


def kernel(x_hbm, gain_hbm, w_in_hbm, w_out_hbm, out_hbm,
           x_v, gain_v, out_v, stat_s, stat_r, z_s, z_g, z_v, w_in_v, w_out_v, d_send, d_recv, own, x_recv, hall,
           acc, e_recv, f_send, f_recv,
           misc_sem, w_in_sem, w_out_sem, stat_sem, z_ssem, z_rsem, d_ssem, d_rsem, x_ssem, x_rsem, y_ssem, y_rsem,
           r_ssem, r_rsem, b_ssem, b_rsem, e_ssem, e_rsem, f_ssem, f_rsem):
    y = lax.axis_index("col")
    row = lax.axis_index("row")
    x = row // 2
    k = row % 2
    dp = lax.axis_index("dp")
    home = 1 - (x + y) % 2
    tok, half = x_v.shape
    feat = half // 2
    block = N * C
    sibling = (dp, y, 2 * x + 1 - k)
    x_next = (dp, y, 2 * (1 - x) + k)
    y_next = (dp, 1 - y, row)

    def remote(src, dst, ssem, rsem, dev):
        return pltpu.make_async_remote_copy(src_ref=src, dst_ref=dst, send_sem=ssem, recv_sem=rsem,
                                            device_id=dev, device_id_type=MESH)

    def col_b(j):
        return C * j

    def col_a(j):
        return C * (NB + j)

    def pos_col(p):
        j = p // 2
        q = p % 2
        is_b = (home + q) % 2
        return is_b * col_b(j) + (1 - is_b) * col_a(j)

    def w_in_copies(p, c):
        cs = pl.multiple_of((1 - k) * block + c, C)
        co = pl.multiple_of(k * block + c, C)
        return (pltpu.make_async_copy(w_in_hbm.at[:, pl.ds(cs, C)], w_in_v.at[p, :, pl.ds(0, C)], w_in_sem.at[p, 0]),
                pltpu.make_async_copy(w_in_hbm.at[:, pl.ds(co, C)], w_in_v.at[p, :, pl.ds(C, C)], w_in_sem.at[p, 1]))

    def w_out_copy(i):
        r = pl.multiple_of(i * C, C)
        return pltpu.make_async_copy(w_out_hbm.at[pl.ds(r, C), :], w_out_v.at[i], w_out_sem.at[i])

    x_copy = pltpu.make_async_copy(x_hbm, x_v, misc_sem.at[0])
    g_copy = pltpu.make_async_copy(gain_hbm, gain_v, misc_sem.at[1])
    x_copy.start()
    g_copy.start()

    def start_pair(p, _):
        for cp in w_in_copies(p, pos_col(p)):
            cp.start()
        return 0

    def start_rest(j, _):
        for cp in w_in_copies(NB + j, col_a(j)):
            cp.start()
        return 0

    lax.fori_loop(0, 2 * NB, start_pair, 0)
    lax.fori_loop(NB, NA, start_rest, 0)

    barrier = pltpu.get_barrier_semaphore()
    for dy in range(2):
        for dr in range(4):
            if dy or dr:
                pl.semaphore_signal(barrier, inc=1, device_id=(dp, (y + dy) % 2, (row + dr) % 4), device_id_type=MESH)

    x_copy.wait()
    g_copy.wait()
    x_f = x_v[...].astype(F32)
    s1 = jnp.sum(x_f, axis=1, keepdims=True)
    s2 = jnp.sum(x_f * x_f, axis=1, keepdims=True)
    lane = lax.broadcasted_iota(jnp.int32, (tok, 128), 1)
    stat_s[...] = jnp.where(lane < 64, s1, s2)
    pl.semaphore_wait(barrier, 7)

    stat_cp = remote(stat_s, stat_r, stat_sem.at[0], stat_sem.at[1], y_next)
    stat_cp.start()
    stat_cp.wait_recv()
    st = (stat_s[...] + stat_r[...]) * (1.0 / (2 * half))
    mean = st[:, 0:1]
    var = st[:, 64:65] - mean * mean
    z = ((x_v[...].astype(F32) - mean) * lax.rsqrt(var + NORM_EPS) * gain_v[...]).astype(BF16)
    z_s[0] = z[:, :feat]
    z_s[1] = z[:, feat:]

    for dy in range(2):
        for dk in range(2):
            ty = (y + dy) % 2
            tk = (k + dk) % 2
            cp = remote(z_s.at[tk], z_g.at[row], z_ssem.at[2 * dy + dk], z_rsem.at[row], (dp, ty, 2 * y + tk))
            if dy == 0 and dk == 0:
                @pl.when(home == 1)
                def _():
                    z_g[row] = z_s[k]

                @pl.when(home == 0)
                def _():
                    cp.start()
            else:
                cp.start()
    for sx in range(2):
        for sk in range(2):
            src = 2 * sx + sk
            cp = remote(z_s.at[0], z_g.at[src], z_ssem.at[0], z_rsem.at[src], y_next)

            @pl.when(1 - home * (1 - (src - row) * (src - row)) > 0)
            def _():
                cp.wait_recv()
    for src in range(4):
        z_v[pl.ds(tok * src, tok), :] = z_g[src]

    acc[...] = jnp.zeros_like(acc)

    def d_copy(p):
        return remote(d_send.at[p], d_recv.at[p], d_ssem.at[p], d_rsem.at[p], sibling)

    def x_copy_of(j, p):
        return remote(own.at[p], x_recv.at[j], x_ssem.at[j], x_rsem.at[j], x_next)

    def up(p, c):
        for cp in w_in_copies(p, c):
            cp.wait()
        part = jnp.dot(z_v[...], w_in_v[p], preferred_element_type=F32)
        d_send[p] = part[:, :C]
        own[p] = part[:, C:]
        d_copy(p).start()

    def pair_sum(p):
        d_copy(p).wait_recv()
        own[p] = own[p] + d_recv[p]

        @pl.when((p < 2 * NB) & (p % 2 == 0))
        def _():
            x_copy_of(p // 2, p).start()

        @pl.when((p >= 2 * NB) & (home == 0))
        def _():
            x_copy_of(p - NB, p).start()

    def up_step(p, _):
        is_pair = (p < 2 * NB).astype(jnp.int32)
        c = is_pair * pos_col(p) + (1 - is_pair) * col_a(p - NB)
        up(p, c)
        w_out_copy(p).start()

        @pl.when(p >= 2)
        def _():
            pair_sum(p - 2)
        return 0

    lax.fori_loop(0, N, up_step, 0)
    pair_sum(N - 2)
    pair_sum(N - 1)

    def y_copy(j):
        return remote(hall.at[j], hall.at[NA + j], y_ssem.at[j], y_rsem.at[j], y_next)

    def relay_copy(j):
        return remote(hall.at[NA + j], hall.at[2 * NA + j], r_ssem.at[j], r_rsem.at[j], x_next)

    def back_copy(j):
        return remote(hall.at[2 * NA + j], hall.at[2 * NA + j], b_ssem.at[j], b_rsem.at[j], y_next)

    def make_h(j):
        x_copy_of(j, 0).wait_recv()
        late = (j >= NB).astype(jnp.int32)
        p = late * (NB + j) + (1 - late) * (2 * j + 1)
        s = own[p] + x_recv[j]
        hall[j] = jax.nn.gelu(s, approximate=True).astype(BF16)
        y_copy(j).start()

    def down(slot, i):
        w_out_copy(i).wait()
        acc[...] += jnp.dot(hall[slot], w_out_v[i], preferred_element_type=F32)

    @pl.when(home == 1)
    def _():
        def relay(i):
            y_copy(i).wait_recv()
            relay_copy(i).start()

        def b_step(i, _):
            back_copy(i).wait_recv()
            down(2 * NA + i, i)
            return 0

        def a_step(j, _):
            @pl.when((j >= 2) & (j < NB + 2))
            def _():
                relay(j - 2)
            make_h(j)
            down(j, NB + j)
            return 0

        lax.fori_loop(0, 10, a_step, 0)

        def mix(m, _):
            lax.fori_loop(2 * m, 2 * m + 2, b_step, 0)
            a_step(10 + m, 0)
            return 0

        lax.fori_loop(0, 2, mix, 0)
        lax.fori_loop(4, NB, b_step, 0)

    @pl.when(home == 0)
    def _():
        def h_step(j, _):
            make_h(j)
            return 0

        def a_step(j, _):
            y_copy(j).wait_recv()
            down(NA + j, NB + j)
            return 0

        def b_step(i, _):
            relay_copy(i).wait_recv()
            back_copy(i).start()
            down(2 * NA + i, i)
            return 0

        def h_a_step(j, _):
            make_h(j + 2)
            a_step(j, 0)
            return 0

        lax.fori_loop(0, 2, h_step, 0)
        lax.fori_loop(0, 6, h_a_step, 0)

        def mix(g, _):
            a_step(6 + g, 0)
            lax.fori_loop(2 * g, 2 * g + 2, b_step, 0)
            return 0

        lax.fori_loop(0, 4, mix, 0)
        lax.fori_loop(10, NA, a_step, 0)

    width = half // TAIL

    def e_copy(t, s):
        tx = s * x + (1 - s) * (1 - x)
        r0 = pl.multiple_of(tok * (2 * tx + 1 - k), 8)
        cols = pl.ds(width * t, width)
        return remote(acc.at[pl.ds(r0, tok), cols], e_recv.at[s, :, cols], e_ssem.at[s, t], e_rsem.at[s, t], sibling)

    def f_copy(t):
        cols = pl.ds(width * t, width)
        return remote(f_send.at[:, cols], f_recv.at[:, cols], f_ssem.at[t], f_rsem.at[t], x_next)

    for t in range(TAIL):
        e_copy(t, 0).start()
    for t in range(TAIL):
        e_copy(t, 1).start()
    far = pl.multiple_of(tok * (2 * (1 - x) + k), 8)
    near = pl.multiple_of(tok * row, 8)
    for t in range(TAIL):
        cols = pl.ds(width * t, width)
        e_copy(t, 0).wait_recv()
        f_send[:, cols] = acc[pl.ds(far, tok), cols] + e_recv[0, :, cols]
        f_copy(t).start()
    for t in range(TAIL):
        cols = pl.ds(width * t, width)
        e_copy(t, 1).wait_recv()
        f_copy(t).wait_recv()
        total = acc[pl.ds(near, tok), cols] + e_recv[1, :, cols] + f_recv[:, cols]
        out_v[:, cols] = (x_v[:, cols].astype(F32) + total).astype(BF16)
    out_copy = pltpu.make_async_copy(out_v, out_hbm, misc_sem.at[2])
    out_copy.start()

    stat_cp.wait_send()
    for dy in range(2):
        for dk in range(2):
            tk = (k + dk) % 2
            cp = remote(z_s.at[tk], z_g.at[row], z_ssem.at[2 * dy + dk], z_rsem.at[row], y_next)
            if dy == 0 and dk == 0:
                @pl.when(home == 0)
                def _():
                    cp.wait_send()
            else:
                cp.wait_send()

    def drain_d(p, _):
        d_copy(p).wait_send()
        return 0

    def drain_xy(j, _):
        x_copy_of(j, 0).wait_send()
        y_copy(j).wait_send()

        @pl.when(home == 1)
        def _():
            relay_copy(j).wait_send()

        @pl.when(home == 0)
        def _():
            back_copy(j).wait_send()
        return 0

    def drain_late_x(j, _):
        @pl.when(home == 0)
        def _():
            x_copy_of(j, 0).wait_send()

        @pl.when(home == 1)
        def _():
            y_copy(j).wait_send()
        return 0

    lax.fori_loop(0, N, drain_d, 0)
    lax.fori_loop(0, NB, drain_xy, 0)
    lax.fori_loop(NB, NA, drain_late_x, 0)
    for t in range(TAIL):
        e_copy(t, 0).wait_send()
        e_copy(t, 1).wait_send()
        f_copy(t).wait_send()
    out_copy.wait()


def solution(mesh):
    def body(x_blk, gain_blk, w_in_blk, w_out_blk):
        tok, half = x_blk.shape
        feat = w_in_blk.shape[0]
        tokens = 4 * tok
        dma = pltpu.SemaphoreType.DMA
        return pl.pallas_call(
            kernel,
            out_shape=jax.ShapeDtypeStruct((tok, half), BF16),
            in_specs=[pl.BlockSpec(memory_space=pl.ANY)] * 4,
            out_specs=pl.BlockSpec(memory_space=pl.ANY),
            scratch_shapes=[
                pltpu.VMEM((tok, half), BF16),
                pltpu.VMEM((1, half), F32),
                pltpu.VMEM((tok, half), BF16),
                pltpu.VMEM((tok, 128), F32),
                pltpu.VMEM((tok, 128), F32),
                pltpu.VMEM((2, tok, feat), BF16),
                pltpu.VMEM((4, tok, feat), BF16),
                pltpu.VMEM((tokens, feat), BF16),
                pltpu.VMEM((N, feat, 2 * C), BF16),
                pltpu.VMEM((N, C, half), BF16),
                pltpu.VMEM((N, tokens, C), F32),
                pltpu.VMEM((N, tokens, C), F32),
                pltpu.VMEM((N, tokens, C), F32),
                pltpu.VMEM((NA, tokens, C), F32),
                pltpu.VMEM((2 * NA + NB, tokens, C), BF16),
                pltpu.VMEM((tokens, half), F32),
                pltpu.VMEM((2, tok, half), F32),
                pltpu.VMEM((tok, half), F32),
                pltpu.VMEM((tok, half), F32),
                dma((3,)),
                dma((N, 2)),
                dma((N,)),
                dma((2,)),
                dma((4,)),
                dma((4,)),
                dma((N,)),
                dma((N,)),
                dma((NA,)),
                dma((NA,)),
                dma((NA,)),
                dma((NA,)),
                dma((NB,)),
                dma((NB,)),
                dma((NB,)),
                dma((NB,)),
                dma((2, TAIL)),
                dma((2, TAIL)),
                dma((TAIL,)),
                dma((TAIL,)),
            ],
            compiler_params=pltpu.CompilerParams(
                collective_id=0, has_side_effects=True, vmem_limit_bytes=67_043_328
            ),
        )(x_blk, gain_blk.reshape(1, half), w_in_blk, w_out_blk)

    return jax.shard_map(
        body,
        mesh=mesh,
        in_specs=(P(("dp", "row"), "col"), P("col"), P("row", "col"), P("row", "col")),
        out_specs=P(("dp", "row"), "col"),
        check_vma=False,
    )
```

time: 151 us -> 59.2 us (0.39)
  Pallas kernels: 0 us -> 56.2 us
  waiting for transfers between devices: 55.8 us -> 0 us
  blocking collectives: 50.2 us -> 0 us
  matrix products: 26.2 us -> 0 us
  between operations: 13.4 us -> 0.01 us
  other arithmetic: 5.21 us -> 0 us
  local copies, waits for them, and re-layouts: 0.09 us -> 2.87 us
    pallas_call x0 -> x1, Pallas kernels: none -> 56.2 us  [body(): pl.pallas_call(kernel, out_shape=jax.ShapeDtypeStruct((tok, half), BF16),...]
    unnamed x4 -> x0, waiting for transfers between devices: 55.8 us -> none
    dot_general x2 -> x0, matrix products: 26.2 us -> none  [the longest x1 14.6 us: local_block(): up_part = jnp.dot(z_cols, w_in_blk, preferred_element_type=jnp.float32)]
    all_to_all x2 -> x0, blocking collectives: 25 us -> none  [the longest x1 16.1 us: local_block(): h_cols = lax.all_to_all(h_rows, 'row', 1, 0, tiled=True)]
    all_gather x2 -> x0, blocking collectives: 18.9 us -> none  [the longest x1 13.4 us: local_block(): h_rows = lax.all_gather(h_blk, 'col', axis=1, tiled=True)]
    psum x1 -> x0, blocking collectives: 6.27 us -> none  [local_block(): row_stats = lax.psum(part_stats, 'col') / d_model]
    convert_element_type x3 -> x0, other arithmetic: 4.14 us -> none  [the longest x1 1.61 us: local_block(): return (x_f32 + down_sum).astype(jnp.bfloat16)]
    unnamed x2 -> x1, local copies, waits for them, and re-layouts: 0.01 us -> 1.56 us
  transfers between devices with their start and end apart: 2 -> 0, of which waited for: 2 -> 0; matrix products, arithmetic and copies ran while one was open for 0% -> 0% of each run, Pallas kernels for 0% -> 0%
where the time goes in v1:
time: 59.2 us; the launch traced here: 59.1 us
  Pallas kernels  56.2 us (95%)
  local copies, waits for them, and re-layouts  2.87 us (5%)
    pallas_call x1, Pallas kernels, body(): pl.pallas_call(kernel, out_shape=jax.ShapeDtypeStruct((tok, half), BF16),...  56.2 us
    unnamed x1, local copies, waits for them, and re-layouts  1.56 us
    reshape x1, local copies, waits for them, and re-layouts, body(): gain_blk.reshape(1, half)  1.31 us

profile of v1, /device:TPU:0, one launch (start us, length us, event | category | flops | bytes accessed | tf_op | source)
XLA Modules:
  0.0 59.1 jit_solution(14397516166201129820)
XLA Ops:
  0.0 1.3 %reshape.3.gain_hbm = f32[1,2560]{1,0:T(1,128)} reshape(f32[2560]{0:T(1024)} %param.5) | data formatting | bytes 20480 | tf_op jit(solution)/shard_map/reshape | solution.py:395
  1.3 56.2 %shard_map.46 = bf16[24,2560]{1,0:T(8,128)(2,1)} custom-call(bf16[24,2560]{1,0:T(8,128)(2,1)} %x_hbm.1, f32[1,2560]{1,0:T(1,128)} %reshape.3.gain_hbm, bf16[1280,10240]{1,0:T(8,128)(2,1)} %w_in_hbm.1, bf16[5120,2560]{1,0:T(8,128)(2,1)} %w_out_hbm.1), custom_call_target="tpu_custom_call" | custom-call | tf_op jit(solution)/shard_map/pallas_call | solution.py:346
  57.5 1.6 %copy.6 = bf16[24,2560]{1,0:T(8,128)(2,1)} copy(bf16[24,2560]{1,0:T(8,128)(2,1)} %shard_map.46) | data formatting | bytes 245760

commit v2 on v1

v2 whole, which is shorter than its diff:
```python
import jax
import jax.numpy as jnp
from jax import lax
from jax.experimental import pallas as pl
from jax.experimental.pallas import tpu as pltpu
from jax.sharding import PartitionSpec as P

NORM_EPS = 1e-5
MESH = pl.DeviceIdType.MESH
F32 = jnp.float32
BF16 = jnp.bfloat16

C = 256
NA = 12
NB = 8
N = NA + NB
GROUP = 5
RING = 8
TAIL = 5


def kernel(x_hbm, gain_hbm, w_in_hbm, w_out_hbm, out_v,
           x_v, gain_v, stat_g, x_g, x_relay, z_v, w_in_v, w_out_v, d_send, d_recv, own, x_recv, hall,
           acc, e_recv, f_send, f_recv,
           misc_sem, w_in_sem, send_sem, d_rsem, x_rsem, y_rsem, b_rsem, e_rsem, f_rsem):
    w_out_sem, stat_rsem, z_rsem = misc_sem.at[4], misc_sem.at[5], misc_sem.at[6]
    stat_ssem, z_ssem, d_ssem, x_ssem, y_ssem, b_ssem, e_ssem, f_ssem = [send_sem.at[i] for i in range(8)]
    y = lax.axis_index("col")
    row = lax.axis_index("row")
    x = row // 2
    k = row % 2
    dp = lax.axis_index("dp")
    home = 1 - (x + y) % 2
    tok, half = x_v.shape
    feat = half // 2
    block = N * C
    sibling = (dp, y, 2 * x + 1 - k)
    x_next = (dp, y, 2 * (1 - x) + k)
    y_next = (dp, 1 - y, row)

    def remote(src, dst, ssem, rsem, dev):
        return pltpu.make_async_remote_copy(src_ref=src, dst_ref=dst, send_sem=ssem, recv_sem=rsem,
                                            device_id=dev, device_id_type=MESH)

    def col_b(j):
        return C * j

    def col_a(j):
        return C * (NB + j)

    def pos_col(p):
        j = p // 2
        q = p % 2
        is_b = (home + q) % 2
        return is_b * col_b(j) + (1 - is_b) * col_a(j)

    def w_in_copies(p, c):
        cs = pl.multiple_of((1 - k) * block + c, C)
        co = pl.multiple_of(k * block + c, C)
        return (pltpu.make_async_copy(w_in_hbm.at[:, pl.ds(cs, C)], w_in_v.at[p, :, pl.ds(0, C)], w_in_sem.at[p // GROUP]),
                pltpu.make_async_copy(w_in_hbm.at[:, pl.ds(co, C)], w_in_v.at[p, :, pl.ds(C, C)], w_in_sem.at[p // GROUP]))

    def w_out_copy(i):
        r = pl.multiple_of(i * C, C)
        return pltpu.make_async_copy(w_out_hbm.at[pl.ds(r, C), :], w_out_v.at[i], w_out_sem)

    x_copy = pltpu.make_async_copy(x_hbm, x_v, misc_sem.at[0])
    g_copy = pltpu.make_async_copy(gain_hbm, gain_v.at[0], misc_sem.at[1])
    x_copy.start()
    g_copy.start()

    def start_pair(p, _):
        for cp in w_in_copies(p, pos_col(p)):
            cp.start()
        return 0

    def start_rest(j, _):
        for cp in w_in_copies(NB + j, col_a(j)):
            cp.start()
        return 0

    lax.fori_loop(0, 2 * NB, start_pair, 0)
    lax.fori_loop(NB, NA, start_rest, 0)

    barrier = pltpu.get_barrier_semaphore()
    for dy in range(2):
        for dr in range(4):
            if dy or dr:
                pl.semaphore_signal(barrier, inc=1, device_id=(dp, (y + dy) % 2, (row + dr) % 4), device_id_type=MESH)

    x_copy.wait()
    g_copy.wait()
    x_f = x_v[...].astype(F32)
    s1 = jnp.sum(x_f, axis=1, keepdims=True)
    s2 = jnp.sum(x_f * x_f, axis=1, keepdims=True)
    lane = lax.broadcasted_iota(jnp.int32, (tok, 128), 1)
    me = 4 * y + row
    stat_g[me, :, :tok] = jnp.transpose(jnp.where(lane == 0, s1, s2))[:8]
    with jax.named_scope('barrier'):
        pl.semaphore_wait(barrier, 7)

    def tok_copy(dy, dk):
        ty = (y + dy) % 2
        tk = (k + dk) % 2
        cols = pl.ds(pl.multiple_of(feat * tk, 128), feat)
        return remote(x_v.at[:, cols], x_g.at[row], z_ssem, z_rsem, (dp, ty, 2 * y + tk))

    def stat_copy(d):
        ty = (y + d // 4) % 2
        tr = (row + d % 4) % 4
        return remote(stat_g.at[me], stat_g.at[me], stat_ssem, stat_rsem, (dp, ty, tr))

    gain_cp = remote(gain_v.at[0], gain_v.at[1], misc_sem.at[2], misc_sem.at[3], y_next)
    half_cols = pl.ds(pl.multiple_of(feat * (1 - k), 128), feat)
    to_relay = remote(x_v.at[:, half_cols], x_relay, z_ssem, misc_sem.at[7], y_next)
    from_relay = remote(x_relay, x_g.at[row], z_ssem, z_rsem, (dp, y, 2 * (1 - x) + 1 - k))

    for d in range(1, 8):
        stat_copy(d).start()

    @pl.when(home == 0)
    def _():
        to_relay.start()
        tok_copy(1, 0).start()
        tok_copy(0, 0).start()
        tok_copy(0, 1).start()

    @pl.when(home == 1)
    def _():
        gain_cp.start()
        tok_copy(0, 1).start()
        tok_copy(1, 0).start()
        tok_copy(1, 1).start()
        x_g[row] = jnp.where(k == 0, x_v[:, :feat], x_v[:, feat:])
        gain_v[1] = gain_v[0]
        with jax.named_scope('x_relay_wait'):
            to_relay.wait_recv()
        from_relay.start()

    @pl.when(home == 0)
    def _():
        with jax.named_scope('gain_wait'):
            gain_cp.wait_recv()
    gain = jnp.where(k == 0, gain_v[1, :feat], gain_v[1, feat:]).reshape(1, feat)
    acc[...] = jnp.zeros_like(acc)
    with jax.named_scope('stat_wait'):
        remote(stat_g.at[pl.ds(0, 7)], stat_g.at[pl.ds(0, 7)], stat_ssem, stat_rsem, y_next).wait_recv()

    @pl.when(home == 0)
    def _():
        with jax.named_scope('z_wait'):
            remote(x_g, x_g, z_ssem, z_rsem, y_next).wait_recv()

    @pl.when(home == 1)
    def _():
        with jax.named_scope('z_wait'):
            remote(x_g.at[pl.ds(0, 3)], x_g.at[pl.ds(0, 3)], z_ssem, z_rsem, y_next).wait_recv()
    for src in range(4):
        st = jnp.transpose(stat_g[src] + stat_g[4 + src])[:tok] * (1.0 / (2 * half))
        mean = st[:, 0:1]
        var = st[:, 1:2] - mean * mean
        z = (x_g[src].astype(F32) - mean) * lax.rsqrt(var + NORM_EPS) * gain
        z_v[pl.ds(tok * src, tok), :] = z.astype(BF16)

    def d_copy(p):
        return remote(d_send.at[p], d_recv.at[p], d_ssem, d_rsem.at[p % RING], sibling)

    def x_copy_of(j, p):
        return remote(own.at[p], x_recv.at[j], x_ssem, x_rsem.at[j], x_next)

    def up(p, c):
        @pl.when(p % GROUP == 0)
        def _():
            with jax.named_scope('w_in_wait'):
                group = w_in_v.at[pl.ds(p, GROUP)]
                pltpu.make_async_copy(group, group, w_in_sem.at[p // GROUP]).wait()

        part = jnp.dot(z_v[...], w_in_v[p], preferred_element_type=F32)
        d_send[p] = part[:, :C]
        own[p] = part[:, C:]
        d_copy(p).start()

    def pair_sum(p):
        with jax.named_scope('pair_wait'):
            d_copy(p).wait_recv()
        own[p] = own[p] + d_recv[p]

        @pl.when((p < 2 * NB) & (p % 2 == 0))
        def _():
            x_copy_of(p // 2, p).start()

        @pl.when((p >= 2 * NB) & (home == 0))
        def _():
            x_copy_of(p - NB, p).start()

    def up_step(p, _):
        is_pair = (p < 2 * NB).astype(jnp.int32)
        c = is_pair * pos_col(p) + (1 - is_pair) * col_a(p - NB)
        up(p, c)
        w_out_copy(p).start()

        @pl.when(p >= 2)
        def _():
            pair_sum(p - 2)
        return 0

    lax.fori_loop(0, N, up_step, 0)
    pair_sum(N - 2)
    pair_sum(N - 1)

    with jax.named_scope('w_out_wait'):
        pltpu.make_async_copy(w_out_v, w_out_v, w_out_sem).wait()

    def y_copy(j):
        return remote(hall.at[j], hall.at[NA + j], y_ssem, y_rsem.at[j], y_next)

    def relay_copy(j):
        return remote(hall.at[NA + j], hall.at[2 * NA + j], b_ssem, b_rsem.at[j], x_next)

    def back_copy(j):
        return remote(hall.at[2 * NA + j], hall.at[2 * NA + j], b_ssem, b_rsem.at[j], y_next)

    def make_h(j):
        with jax.named_scope('x_wait'):
            x_copy_of(j, 0).wait_recv()
        late = (j >= NB).astype(jnp.int32)
        p = late * (NB + j) + (1 - late) * (2 * j + 1)
        s = own[p] + x_recv[j]
        hall[j] = jax.nn.gelu(s, approximate=True).astype(BF16)
        y_copy(j).start()

    def down(slot, i):
        acc[...] += jnp.dot(hall[slot], w_out_v[i], preferred_element_type=F32)

    @pl.when(home == 1)
    def _():
        def relay(i):
            with jax.named_scope('relay_wait'):
                y_copy(i).wait_recv()
            relay_copy(i).start()

        def b_step(i, _):
            with jax.named_scope('b_wait'):
                back_copy(i).wait_recv()
            down(2 * NA + i, i)
            return 0

        def a_step(j, _):
            @pl.when((j >= 2) & (j < NB + 2))
            def _():
                relay(j - 2)
            make_h(j)
            down(j, NB + j)
            return 0

        lax.fori_loop(0, 10, a_step, 0)

        def mix(m, _):
            lax.fori_loop(2 * m, 2 * m + 2, b_step, 0)
            a_step(10 + m, 0)
            return 0

        lax.fori_loop(0, 2, mix, 0)
        lax.fori_loop(4, NB, b_step, 0)

    @pl.when(home == 0)
    def _():
        def h_step(j, _):
            make_h(j)
            return 0

        def a_step(j, _):
            with jax.named_scope('a_wait'):
                y_copy(j).wait_recv()
            down(NA + j, NB + j)
            return 0

        def b_step(i, _):
            with jax.named_scope('b_wait'):
                relay_copy(i).wait_recv()
            back_copy(i).start()
            down(2 * NA + i, i)
            return 0

        def h_a_step(j, _):
            make_h(j + 2)
            a_step(j, 0)
            return 0

        lax.fori_loop(0, 2, h_step, 0)
        lax.fori_loop(0, 6, h_a_step, 0)

        def mix(g, _):
            a_step(6 + g, 0)
            lax.fori_loop(2 * g, 2 * g + 2, b_step, 0)
            return 0

        lax.fori_loop(0, 4, mix, 0)
        lax.fori_loop(10, NA, a_step, 0)

    width = half // TAIL

    def e_copy(t, s):
        tx = s * x + (1 - s) * (1 - x)
        r0 = pl.multiple_of(tok * (2 * tx + 1 - k), 8)
        cols = pl.ds(width * t, width)
        return remote(acc.at[pl.ds(r0, tok), cols], e_recv.at[s, :, cols], e_ssem, e_rsem.at[s, t], sibling)

    def f_copy(t):
        cols = pl.ds(width * t, width)
        return remote(f_send.at[:, cols], f_recv.at[:, cols], f_ssem, f_rsem.at[t], x_next)

    for t in range(TAIL):
        e_copy(t, 0).start()
    for t in range(TAIL):
        e_copy(t, 1).start()
    far = pl.multiple_of(tok * (2 * (1 - x) + k), 8)
    near = pl.multiple_of(tok * row, 8)
    for t in range(TAIL):
        cols = pl.ds(width * t, width)
        with jax.named_scope('e0_wait'):
            e_copy(t, 0).wait_recv()
        f_send[:, cols] = acc[pl.ds(far, tok), cols] + e_recv[0, :, cols]
        f_copy(t).start()
    def sent(ref, sem):
        remote(ref, ref, sem, sem, y_next).wait_send()

    with jax.named_scope('drain'):
        sent(stat_g.at[pl.ds(0, 7)], stat_ssem)
        sent(x_g, z_ssem)
        sent(d_send, d_ssem)
        sent(hall.at[pl.ds(0, NB)], b_ssem)
        sent(e_recv, e_ssem)

        @pl.when(home == 0)
        def _():
            sent(own.at[pl.ds(0, NA)], x_ssem)
            sent(hall.at[pl.ds(0, NB)], y_ssem)

        @pl.when(home == 1)
        def _():
            gain_cp.wait_send()
            sent(own.at[pl.ds(0, NB)], x_ssem)
            sent(hall.at[pl.ds(0, NA)], y_ssem)

    for t in range(TAIL):
        cols = pl.ds(width * t, width)
        with jax.named_scope('e1_wait'):
            e_copy(t, 1).wait_recv()
        with jax.named_scope('f_wait'):
            f_copy(t).wait_recv()
        total = acc[pl.ds(near, tok), cols] + e_recv[1, :, cols] + f_recv[:, cols]
        out_v[:, cols] = (x_v[:, cols].astype(F32) + total).astype(BF16)
    sent(f_send, f_ssem)


def solution(mesh):
    def body(x_blk, gain_blk, w_in_blk, w_out_blk):
        tok, half = x_blk.shape
        feat = w_in_blk.shape[0]
        tokens = 4 * tok
        dma = pltpu.SemaphoreType.DMA
        return pl.pallas_call(
            kernel,
            out_shape=pltpu.VMEM((tok, half), BF16),
            in_specs=[pl.BlockSpec(memory_space=pl.ANY)] * 4,
            out_specs=pl.BlockSpec(memory_space=pltpu.VMEM),
            scratch_shapes=[
                pltpu.VMEM((tok, half), BF16),
                pltpu.VMEM((2, half), F32),
                pltpu.VMEM((8, 8, 128), F32),
                pltpu.VMEM((4, tok, feat), BF16),
                pltpu.VMEM((tok, feat), BF16),
                pltpu.VMEM((tokens, feat), BF16),
                pltpu.VMEM((N, feat, 2 * C), BF16),
                pltpu.VMEM((N, C, half), BF16),
                pltpu.VMEM((N, tokens, C), F32),
                pltpu.VMEM((N, tokens, C), F32),
                pltpu.VMEM((N, tokens, C), F32),
                pltpu.VMEM((NA, tokens, C), F32),
                pltpu.VMEM((2 * NA + NB, tokens, C), BF16),
                pltpu.VMEM((tokens, half), F32),
                pltpu.VMEM((2, tok, half), F32),
                pltpu.VMEM((tok, half), F32),
                pltpu.VMEM((tok, half), F32),
                dma((8,)),
                dma((N // GROUP,)),
                dma((8,)),
                dma((RING,)),
                dma((NA,)),
                dma((NA,)),
                dma((NB,)),
                dma((2, TAIL)),
                dma((TAIL,)),
            ],
            compiler_params=pltpu.CompilerParams(
                collective_id=0, has_side_effects=True, vmem_limit_bytes=66_500_000
            ),
        )(x_blk, gain_blk, w_in_blk, w_out_blk)

    return jax.shard_map(
        body,
        mesh=mesh,
        in_specs=(P(("dp", "row"), "col"), P("col"), P("row", "col"), P("row", "col")),
        out_specs=P(("dp", "row"), "col"),
        check_vma=False,
    )
```

time: 59.2 us -> 53.2 us (0.90)
  Pallas kernels: 56.2 us -> 52.4 us
  local copies, waits for them, and re-layouts: 2.87 us -> 0.65 us
    pallas_call x1, Pallas kernels: 56.2 us -> 52.4 us  [body(): pl.pallas_call(kernel, out_shape=pltpu.VMEM((tok, half), BF16), in_specs=...]
    reshape x1 -> x0, local copies, waits for them, and re-layouts: 1.31 us -> none  [body(): gain_blk.reshape(1, half)]
    unnamed x1, local copies, waits for them, and re-layouts: 1.56 us -> 0.65 us
where the time goes in v2:
time: 53.2 us; the launch traced here: 53.1 us
  Pallas kernels  52.4 us (98%)
  local copies, waits for them, and re-layouts  0.65 us (1%)
    pallas_call x1, Pallas kernels, body(): pl.pallas_call(kernel, out_shape=pltpu.VMEM((tok, half), BF16), in_specs=...  52.4 us

profile of v2, /device:TPU:0, one launch (start us, length us, event | category | flops | bytes accessed | tf_op | source)
XLA Modules:
  0.0 53.1 jit_solution(1034877636168352163)
XLA Ops:
  0.0 52.4 %shard_map.46 = bf16[24,2560]{1,0:T(8,128)(2,1)S(1)} custom-call(bf16[24,2560]{1,0:T(8,128)(2,1)} %x_hbm.1, f32[2560]{0:T(1024)} %gain_hbm.1, bf16[1280,10240]{1,0:T(8,128)(2,1)} %w_in_hbm.1, bf16[5120,2560]{1,0:T(8,128)(2,1)} %w_out_hbm.1), custom_call_target="tpu_custom_call" | custom-call | tf_op jit(solution)/shard_map/pallas_call | solution.py:363
  52.4 0.7 %copy.6 = bf16[24,2560]{1,0:T(8,128)(2,1)} copy(bf16[24,2560]{1,0:T(8,128)(2,1)S(1)} %shard_map.46) | data formatting | bytes 245760

commit v3 on v2

--- a/solution.py
+++ b/solution.py
@@ -14,14 +14,15 @@
 NA = 12
 NB = 8
 N = NA + NB
+NF = 4
 GROUP = 5
 RING = 8
-TAIL = 5
+TA = 16
 
 
 def kernel(x_hbm, gain_hbm, w_in_hbm, w_out_hbm, out_v,
            x_v, gain_v, stat_g, x_g, x_relay, z_v, w_in_v, w_out_v, d_send, d_recv, own, x_recv, hall,
-           acc, e_recv, f_send, f_recv,
+           acc, ea_recv, eb_recv, fa_send, fa_recv, fb_send, fb_recv,
            misc_sem, w_in_sem, send_sem, d_rsem, x_rsem, y_rsem, b_rsem, e_rsem, f_rsem):
     w_out_sem, stat_rsem, z_rsem = misc_sem.at[4], misc_sem.at[5], misc_sem.at[6]
     stat_ssem, z_ssem, d_ssem, x_ssem, y_ssem, b_ssem, e_ssem, f_ssem = [send_sem.at[i] for i in range(8)]
@@ -34,6 +35,9 @@
     tok, half = x_v.shape
     feat = half // 2
     block = N * C
+    rows_a = 4 * TA
+    tb = tok - TA
+    rows_b = 4 * tb
     sibling = (dp, y, 2 * x + 1 - k)
     x_next = (dp, y, 2 * (1 - x) + k)
     y_next = (dp, 1 - y, row)
@@ -69,24 +73,24 @@
     x_copy.start()
     g_copy.start()
 
-    def start_pair(p, _):
-        for cp in w_in_copies(p, pos_col(p)):
-            cp.start()
-        return 0
-
-    def start_rest(j, _):
-        for cp in w_in_copies(NB + j, col_a(j)):
-            cp.start()
-        return 0
-
-    lax.fori_loop(0, 2 * NB, start_pair, 0)
-    lax.fori_loop(NB, NA, start_rest, 0)
-
     barrier = pltpu.get_barrier_semaphore()
     for dy in range(2):
         for dr in range(4):
             if dy or dr:
                 pl.semaphore_signal(barrier, inc=1, device_id=(dp, (y + dy) % 2, (row + dr) % 4), device_id_type=MESH)
+
+    def start_pair(p, _):
+        for cp in w_in_copies(p, pos_col(p)):
+            cp.start()
+        return 0
+
+    def start_rest(j, _):
+        for cp in w_in_copies(NB + j, col_a(j)):
+            cp.start()
+        return 0
+
+    lax.fori_loop(0, 2 * NB, start_pair, 0)
+    lax.fori_loop(NB, NA, start_rest, 0)
 
     x_copy.wait()
     g_copy.wait()
@@ -160,13 +164,29 @@
         mean = st[:, 0:1]
         var = st[:, 1:2] - mean * mean
         z = (x_g[src].astype(F32) - mean) * lax.rsqrt(var + NORM_EPS) * gain
-        z_v[pl.ds(tok * src, tok), :] = z.astype(BF16)
+        z = z.astype(BF16)
+        z_v[pl.ds(TA * src, TA), :] = z[:TA]
+        z_v[pl.ds(rows_a + tb * src, tb), :] = z[TA:]
 
     def d_copy(p):
         return remote(d_send.at[p], d_recv.at[p], d_ssem, d_rsem.at[p % RING], sibling)
 
-    def x_copy_of(j, p):
-        return remote(own.at[p], x_recv.at[j], x_ssem, x_rsem.at[j], x_next)
+    def slot_of(p):
+        late = p // (2 * NB)
+        return (1 - late) * (p // 2 + NA * (p % 2)) + late * (p - NB + NA * home)
+
+    row_group = (pl.ds(0, rows_a), pl.ds(rows_a, rows_b))
+
+    def part_of(ref, j, part):
+        if part == 2:
+            return ref.at[j]
+        if part == 0:
+            return ref.at[j, row_group[0]]
+        return ref.at[pl.ds(j, 2), row_group[1]]
+
+    def x_copy_of(j, part):
+        sem = x_rsem.at[NA + j // 2] if part == 1 else x_rsem.at[j]
+        return remote(part_of(own, j, part), part_of(x_recv, j, part), x_ssem, sem, x_next)
 
     def up(p, c):
         @pl.when(p % GROUP == 0)
@@ -177,26 +197,26 @@
 
         part = jnp.dot(z_v[...], w_in_v[p], preferred_element_type=F32)
         d_send[p] = part[:, :C]
-        own[p] = part[:, C:]
+        own[slot_of(p)] = part[:, C:]
         d_copy(p).start()
 
     def pair_sum(p):
         with jax.named_scope('pair_wait'):
             d_copy(p).wait_recv()
-        own[p] = own[p] + d_recv[p]
-
-        @pl.when((p < 2 * NB) & (p % 2 == 0))
-        def _():
-            x_copy_of(p // 2, p).start()
-
-        @pl.when((p >= 2 * NB) & (home == 0))
-        def _():
-            x_copy_of(p - NB, p).start()
+        slot = slot_of(p)
+        own[slot] = own[slot] + d_recv[p]
+
+        @pl.when((slot < NA) & ((home == 1) | (slot >= NF)))
+        def _():
+            x_copy_of(slot, 0).start()
+
+        @pl.when((slot < NF) & (home == 0))
+        def _():
+            x_copy_of(slot, 2).start()
 
     def up_step(p, _):
-        is_pair = (p < 2 * NB).astype(jnp.int32)
-        c = is_pair * pos_col(p) + (1 - is_pair) * col_a(p - NB)
-        up(p, c)
+        late = p // (2 * NB)
+        up(p, (1 - late) * pos_col(p) + late * col_a(p - NB))
         w_out_copy(p).start()
 
         @pl.when(p >= 2)
@@ -208,120 +228,181 @@
     pair_sum(N - 2)
     pair_sum(N - 1)
 
+    first_b = NF * (1 - home)
+    for m in range(NB // 2):
+        x_copy_of(first_b + 2 * m, 1).start()
+
     with jax.named_scope('w_out_wait'):
         pltpu.make_async_copy(w_out_v, w_out_v, w_out_sem).wait()
 
-    def y_copy(j):
-        return remote(hall.at[j], hall.at[NA + j], y_ssem, y_rsem.at[j], y_next)
-
-    def relay_copy(j):
-        return remote(hall.at[NA + j], hall.at[2 * NA + j], b_ssem, b_rsem.at[j], x_next)
-
-    def back_copy(j):
-        return remote(hall.at[2 * NA + j], hall.at[2 * NA + j], b_ssem, b_rsem.at[j], y_next)
-
-    def make_h(j):
+    def y_copy(j, part):
+        sem = y_rsem.at[NA + j // 2] if part == 1 else y_rsem.at[j]
+        return remote(part_of(hall, j, part), part_of(hall, NA + j, part), y_ssem, sem, y_next)
+
+    def b_sem(j, part):
+        return b_rsem.at[NB + j // 2] if part == 1 else b_rsem.at[j]
+
+    def relay_copy(j, part):
+        return remote(part_of(hall, NA + j, part), part_of(hall, 2 * NA + j, part), b_ssem, b_sem(j, part), x_next)
+
+    def back_copy(j, part):
+        return remote(part_of(hall, 2 * NA + j, part), part_of(hall, 2 * NA + j, part), b_ssem, b_sem(j, part), y_next)
+
+    def make_h(j, part):
         with jax.named_scope('x_wait'):
-            x_copy_of(j, 0).wait_recv()
-        late = (j >= NB).astype(jnp.int32)
-        p = late * (NB + j) + (1 - late) * (2 * j + 1)
-        s = own[p] + x_recv[j]
-        hall[j] = jax.nn.gelu(s, approximate=True).astype(BF16)
-        y_copy(j).start()
-
-    def down(slot, i):
-        acc[...] += jnp.dot(hall[slot], w_out_v[i], preferred_element_type=F32)
+            x_copy_of(j, part).wait_recv()
+        if part == 2:
+            rows, chunks = pl.ds(0, rows_a + rows_b), (j,)
+        elif part == 0:
+            rows, chunks = row_group[0], (j,)
+        else:
+            rows, chunks = row_group[1], (j, j + 1)
+        for c in chunks:
+            total = own[NA + c, rows, :] + x_recv[c, rows, :]
+            hall[c, rows, :] = jax.nn.gelu(total, approximate=True).astype(BF16)
+        y_copy(j, part).start()
+
+    def down(slot, i, part):
+        if part == 2:
+            acc[...] += jnp.dot(hall[slot], w_out_v[i], preferred_element_type=F32)
+        elif part == 0:
+            rows = row_group[0]
+            acc[rows, :] += jnp.dot(hall[slot, rows, :], w_out_v[i], preferred_element_type=F32)
+        else:
+            rows = row_group[1]
+            acc[rows, :] += (jnp.dot(hall[slot, rows, :], w_out_v[i], preferred_element_type=F32)
+                             + jnp.dot(hall[slot + 1, rows, :], w_out_v[i + 1], preferred_element_type=F32))
+
+    e_recv, f_send, f_recv = (ea_recv, eb_recv), (fa_send, fb_send), (fa_recv, fb_recv)
+
+    def token_rows(group, r):
+        n, base = ((TA, 0), (tb, rows_a))[group]
+        return pl.ds(pl.multiple_of(base + n * r, 8), n)
+
+    def e_copy(group, s):
+        r = 2 * (s * x + (1 - s) * (1 - x)) + 1 - k
+        return remote(acc.at[token_rows(group, r)], e_recv[group].at[s], e_ssem, e_rsem.at[2 * group + s], sibling)
+
+    def f_copy(group):
+        return remote(f_send[group], f_recv[group], f_ssem, f_rsem.at[group], x_next)
+
+    def end_start(group):
+        e_copy(group, 0).start()
+        e_copy(group, 1).start()
+
+    def end_send(group):
+        with jax.named_scope('e0_wait'):
+            e_copy(group, 0).wait_recv()
+        f_send[group][...] = acc[token_rows(group, 2 * (1 - x) + k), :] + e_recv[group][0]
+        f_copy(group).start()
+
+    def end_sum(group):
+        with jax.named_scope('e1_wait'):
+            e_copy(group, 1).wait_recv()
+        with jax.named_scope('f_wait'):
+            f_copy(group).wait_recv()
+        total = acc[token_rows(group, row), :] + e_recv[group][1] + f_recv[group][...]
+        t0, n = ((0, TA), (TA, tb))[group]
+        out_v[t0:t0 + n, :] = (x_v[t0:t0 + n, :].astype(F32) + total).astype(BF16)
+
+    def loop(lo, hi, step):
+        def body(i, _):
+            step(i)
+            return 0
+        lax.fori_loop(lo, hi, body, 0)
 
     @pl.when(home == 1)
     def _():
-        def relay(i):
+        def relay(i, part):
             with jax.named_scope('relay_wait'):
-                y_copy(i).wait_recv()
-            relay_copy(i).start()
-
-        def b_step(i, _):
+                y_copy(i, part).wait_recv()
+            relay_copy(i, part).start()
+
+        def b_step(i, part):
             with jax.named_scope('b_wait'):
-                back_copy(i).wait_recv()
-            down(2 * NA + i, i)
-            return 0
-
-        def a_step(j, _):
-            @pl.when((j >= 2) & (j < NB + 2))
+                back_copy(i, part).wait_recv()
+            down(2 * NA + i, i, part)
+
+        def a_step(j, part):
+            make_h(j, part)
+            down(j, NB + j, part)
+
+        loop(0, NF, lambda j: a_step(j, 2))
+
+        def step(t):
+            @pl.when((t >= 1) & (t < 5))
             def _():
-                relay(j - 2)
-            make_h(j)
-            down(j, NB + j)
-            return 0
-
-        lax.fori_loop(0, 10, a_step, 0)
-
-        def mix(m, _):
-            lax.fori_loop(2 * m, 2 * m + 2, b_step, 0)
-            a_step(10 + m, 0)
-            return 0
-
-        lax.fori_loop(0, 2, mix, 0)
-        lax.fori_loop(4, NB, b_step, 0)
+                relay(2 * t - 2, 0)
+                relay(2 * t - 1, 0)
+
+            @pl.when(t >= 5)
+            def _():
+                relay(2 * (t - 5), 1)
+            a_step(NF + t, 0)
+
+        loop(0, NA - NF, step)
+        relay(NB - 2, 1)
+
+        def step(m):
+            b_step(2 * m, 0)
+            a_step(NF + 2 * m, 1)
+            b_step(2 * m + 1, 0)
+
+        loop(0, NB // 2, step)
+        end_start(0)
+        loop(0, 1, lambda m: b_step(2 * m, 1))
+        end_send(0)
+        loop(1, NB // 2, lambda m: b_step(2 * m, 1))
 
     @pl.when(home == 0)
     def _():
-        def h_step(j, _):
-            make_h(j)
-            return 0
-
-        def a_step(j, _):
+        def a_step(j, part):
             with jax.named_scope('a_wait'):
-                y_copy(j).wait_recv()
-            down(NA + j, NB + j)
-            return 0
-
-        def b_step(i, _):
+                y_copy(j, part).wait_recv()
+            down(NA + j, NB + j, part)
+
+        def b_step(i, part):
             with jax.named_scope('b_wait'):
-                relay_copy(i).wait_recv()
-            back_copy(i).start()
-            down(2 * NA + i, i)
-            return 0
-
-        def h_a_step(j, _):
-            make_h(j + 2)
-            a_step(j, 0)
-            return 0
-
-        lax.fori_loop(0, 2, h_step, 0)
-        lax.fori_loop(0, 6, h_a_step, 0)
-
-        def mix(g, _):
-            a_step(6 + g, 0)
-            lax.fori_loop(2 * g, 2 * g + 2, b_step, 0)
-            return 0
-
-        lax.fori_loop(0, 4, mix, 0)
-        lax.fori_loop(10, NA, a_step, 0)
-
-    width = half // TAIL
-
-    def e_copy(t, s):
-        tx = s * x + (1 - s) * (1 - x)
-        r0 = pl.multiple_of(tok * (2 * tx + 1 - k), 8)
-        cols = pl.ds(width * t, width)
-        return remote(acc.at[pl.ds(r0, tok), cols], e_recv.at[s, :, cols], e_ssem, e_rsem.at[s, t], sibling)
-
-    def f_copy(t):
-        cols = pl.ds(width * t, width)
-        return remote(f_send.at[:, cols], f_recv.at[:, cols], f_ssem, f_rsem.at[t], x_next)
-
-    for t in range(TAIL):
-        e_copy(t, 0).start()
-    for t in range(TAIL):
-        e_copy(t, 1).start()
-    far = pl.multiple_of(tok * (2 * (1 - x) + k), 8)
-    near = pl.multiple_of(tok * row, 8)
-    for t in range(TAIL):
-        cols = pl.ds(width * t, width)
-        with jax.named_scope('e0_wait'):
-            e_copy(t, 0).wait_recv()
-        f_send[:, cols] = acc[pl.ds(far, tok), cols] + e_recv[0, :, cols]
-        f_copy(t).start()
+                relay_copy(i, part).wait_recv()
+            back_copy(i, part).start()
+            down(2 * NA + i, i, part)
+
+        loop(0, NB, lambda j: make_h(j, 0))
+
+        def step(t):
+            a_step(2 * t, 2)
+            a_step(2 * t + 1, 2)
+            make_h(2 * t, 1)
+
+        loop(0, 2, step)
+
+        def step(t):
+            a_step(NF + 2 * t, 0)
+            make_h(4 + 2 * t, 1)
+            a_step(NF + 2 * t + 1, 0)
+
+        loop(0, 2, step)
+
+        def step(t):
+            b_step(2 * t, 0)
+            b_step(2 * t + 1, 0)
+            a_step(NF + 4 + t, 0)
+
+        loop(0, 4, step)
+        end_start(0)
+        loop(0, 2, lambda m: b_step(2 * m, 1))
+        end_send(0)
+
+        def step(m):
+            b_step(4 + 2 * m, 1)
+            a_step(NF + 2 * m, 1)
+
+        loop(0, 2, step)
+        loop(2, 4, lambda m: a_step(NF + 2 * m, 1))
+
+    end_start(1)
+    end_send(1)
+
     def sent(ref, sem):
         remote(ref, ref, sem, sem, y_next).wait_send()
 
@@ -330,7 +411,8 @@
         sent(x_g, z_ssem)
         sent(d_send, d_ssem)
         sent(hall.at[pl.ds(0, NB)], b_ssem)
-        sent(e_recv, e_ssem)
+        sent(ea_recv, e_ssem)
+        sent(eb_recv, e_ssem)
 
         @pl.when(home == 0)
         def _():
@@ -343,15 +425,10 @@
             sent(own.at[pl.ds(0, NB)], x_ssem)
             sent(hall.at[pl.ds(0, NA)], y_ssem)
 
-    for t in range(TAIL):
-        cols = pl.ds(width * t, width)
-        with jax.named_scope('e1_wait'):
-            e_copy(t, 1).wait_recv()
-        with jax.named_scope('f_wait'):
-            f_copy(t).wait_recv()
-        total = acc[pl.ds(near, tok), cols] + e_recv[1, :, cols] + f_recv[:, cols]
-        out_v[:, cols] = (x_v[:, cols].astype(F32) + total).astype(BF16)
-    sent(f_send, f_ssem)
+    end_sum(0)
+    end_sum(1)
+    sent(fa_send, f_ssem)
+    sent(fb_send, f_ssem)
 
 
 def solution(mesh):
@@ -376,22 +453,25 @@
                 pltpu.VMEM((N, C, half), BF16),
                 pltpu.VMEM((N, tokens, C), F32),
                 pltpu.VMEM((N, tokens, C), F32),
-                pltpu.VMEM((N, tokens, C), F32),
+                pltpu.VMEM((2 * NA, tokens, C), F32),
                 pltpu.VMEM((NA, tokens, C), F32),
                 pltpu.VMEM((2 * NA + NB, tokens, C), BF16),
                 pltpu.VMEM((tokens, half), F32),
-                pltpu.VMEM((2, tok, half), F32),
-                pltpu.VMEM((tok, half), F32),
-                pltpu.VMEM((tok, half), F32),
+                pltpu.VMEM((2, TA, half), F32),
+                pltpu.VMEM((2, tok - TA, half), F32),
+                pltpu.VMEM((TA, half), F32),
+                pltpu.VMEM((TA, half), F32),
+                pltpu.VMEM((tok - TA, half), F32),
+                pltpu.VMEM((tok - TA, half), F32),
                 dma((8,)),
                 dma((N // GROUP,)),
                 dma((8,)),
                 dma((RING,)),
-                dma((NA,)),
-                dma((NA,)),
-                dma((NB,)),
-                dma((2, TAIL)),
-                dma((TAIL,)),
+                dma((NA + NA // 2,)),
+                dma((NA + NA // 2,)),
+                dma((NB + NB // 2,)),
+                dma((4,)),
+                dma((2,)),
             ],
             compiler_params=pltpu.CompilerParams(
                 collective_id=0, has_side_effects=True, vmem_limit_bytes=66_500_000

time: 53.2 us -> 48.7 us (0.915)
  Pallas kernels: 52.4 us -> 47.9 us
    pallas_call x1, Pallas kernels: 52.4 us -> 47.9 us  [body(): pl.pallas_call(kernel, out_shape=pltpu.VMEM((tok, half), BF16), in_specs=...]
where the time goes in v3:
time: 48.7 us; the launch traced here: 48.6 us
  Pallas kernels  47.9 us (98%)
  local copies, waits for them, and re-layouts  0.65 us (1%)
    pallas_call x1, Pallas kernels, body(): pl.pallas_call(kernel, out_shape=pltpu.VMEM((tok, half), BF16), in_specs=...  47.9 us

profile of v3, /device:TPU:0, one launch (start us, length us, event | category | flops | bytes accessed | tf_op | source)
XLA Modules:
  0.0 48.6 jit_solution(16078784483324225787)
XLA Ops:
  0.0 47.9 %shard_map.46 = bf16[24,2560]{1,0:T(8,128)(2,1)S(1)} custom-call(bf16[24,2560]{1,0:T(8,128)(2,1)} %x_hbm.1, f32[2560]{0:T(1024)} %gain_hbm.1, bf16[1280,10240]{1,0:T(8,128)(2,1)} %w_in_hbm.1, bf16[5120,2560]{1,0:T(8,128)(2,1)} %w_out_hbm.1), custom_call_target="tpu_custom_call" | custom-call | tf_op jit(solution)/shard_map/pallas_call | solution.py:440
  47.9 0.7 %copy.6 = bf16[24,2560]{1,0:T(8,128)(2,1)} copy(bf16[24,2560]{1,0:T(8,128)(2,1)S(1)} %shard_map.46) | data formatting | bytes 245760

commit v4 on v3

--- a/solution.py
+++ b/solution.py
@@ -11,21 +11,22 @@
 BF16 = jnp.bfloat16
 
 C = 256
-NA = 12
-NB = 8
-N = NA + NB
-NF = 4
+NB = 4
+NC = 5
+NA = 11
+N = NA + NB + NC
+NF = 3
 GROUP = 5
 RING = 8
 TA = 16
 
 
 def kernel(x_hbm, gain_hbm, w_in_hbm, w_out_hbm, out_v,
-           x_v, gain_v, stat_g, x_g, x_relay, z_v, w_in_v, w_out_v, d_send, d_recv, own, x_recv, hall,
+           x_v, gain_v, stat_g, x_g, x_relay, z_v, w_in_v, w_out_v, d_send, d_recv, own, x_recv, c_recv, hall,
            acc, ea_recv, eb_recv, fa_send, fa_recv, fb_send, fb_recv,
-           misc_sem, w_in_sem, send_sem, d_rsem, x_rsem, y_rsem, b_rsem, e_rsem, f_rsem):
+           misc_sem, w_in_sem, send_sem, d_rsem, x_rsem, y_rsem, b_rsem, c_rsem, e_rsem, f_rsem):
     w_out_sem, stat_rsem, z_rsem = misc_sem.at[4], misc_sem.at[5], misc_sem.at[6]
-    stat_ssem, z_ssem, d_ssem, x_ssem, y_ssem, b_ssem, e_ssem, f_ssem = [send_sem.at[i] for i in range(8)]
+    stat_ssem, z_ssem, d_ssem, x_ssem, y_ssem, b_ssem, c_ssem, e_ssem, f_ssem = [send_sem.at[i] for i in range(9)]
     y = lax.axis_index("col")
     row = lax.axis_index("row")
     x = row // 2
@@ -46,19 +47,17 @@
         return pltpu.make_async_remote_copy(src_ref=src, dst_ref=dst, send_sem=ssem, recv_sem=rsem,
                                             device_id=dev, device_id_type=MESH)
 
-    def col_b(j):
-        return C * j
-
-    def col_a(j):
-        return C * (NB + j)
-
-    def pos_col(p):
-        j = p // 2
-        q = p % 2
-        is_b = (home + q) % 2
-        return is_b * col_b(j) + (1 - is_b) * col_a(j)
-
-    def w_in_copies(p, c):
+    c0, a0 = NB, NB + NC
+
+    def chunk_of(p):
+        u = p - 2 * NB - 1
+        pair = jnp.where(p % 2 == 1, c0 + p // 2, p // 2 + (1 - home) * a0)
+        mixed = jnp.where(u % 2 == 1, u // 2, a0 + NB + u // 2)
+        late = jnp.where((home == 1) | (u >= 2 * NB), a0 + u, mixed)
+        return jnp.where(p < 2 * NB, pair, jnp.where(u < 0, a0 - 1, late))
+
+    def w_in_copies(p):
+        c = C * chunk_of(p)
         cs = pl.multiple_of((1 - k) * block + c, C)
         co = pl.multiple_of(k * block + c, C)
         return (pltpu.make_async_copy(w_in_hbm.at[:, pl.ds(cs, C)], w_in_v.at[p, :, pl.ds(0, C)], w_in_sem.at[p // GROUP]),
@@ -79,18 +78,12 @@
             if dy or dr:
                 pl.semaphore_signal(barrier, inc=1, device_id=(dp, (y + dy) % 2, (row + dr) % 4), device_id_type=MESH)
 
-    def start_pair(p, _):
-        for cp in w_in_copies(p, pos_col(p)):
+    def start_w_in(p, _):
+        for cp in w_in_copies(p):
             cp.start()
         return 0
 
-    def start_rest(j, _):
-        for cp in w_in_copies(NB + j, col_a(j)):
-            cp.start()
-        return 0
-
-    lax.fori_loop(0, 2 * NB, start_pair, 0)
-    lax.fori_loop(NB, NA, start_rest, 0)
+    lax.fori_loop(0, N, start_w_in, 0)
 
     x_copy.wait()
     g_copy.wait()
@@ -171,10 +164,6 @@
     def d_copy(p):
         return remote(d_send.at[p], d_recv.at[p], d_ssem, d_rsem.at[p % RING], sibling)
 
-    def slot_of(p):
-        late = p // (2 * NB)
-        return (1 - late) * (p // 2 + NA * (p % 2)) + late * (p - NB + NA * home)
-
     row_group = (pl.ds(0, rows_a), pl.ds(rows_a, rows_b))
 
     def part_of(ref, j, part):
@@ -184,11 +173,22 @@
             return ref.at[j, row_group[0]]
         return ref.at[pl.ds(j, 2), row_group[1]]
 
-    def x_copy_of(j, part):
+    def x_copy_of(j, part, first):
         sem = x_rsem.at[NA + j // 2] if part == 1 else x_rsem.at[j]
-        return remote(part_of(own, j, part), part_of(x_recv, j, part), x_ssem, sem, x_next)
-
-    def up(p, c):
+        return remote(part_of(own, first + j, part), part_of(x_recv, j, part), x_ssem, sem, x_next)
+
+    def c_copy(j):
+        return remote(own.at[c0 + j], c_recv.at[0, j], c_ssem, c_rsem.at[j], y_next)
+
+    def c_relay(j):
+        return remote(c_recv.at[0, j], c_recv.at[1, j], c_ssem, c_rsem.at[NC + j], x_next)
+
+    def pass_c(j):
+        with jax.named_scope('c_wait'):
+            c_copy(j).wait_recv()
+        c_relay(j).start()
+
+    def up(p):
         @pl.when(p % GROUP == 0)
         def _():
             with jax.named_scope('w_in_wait'):
@@ -197,40 +197,56 @@
 
         part = jnp.dot(z_v[...], w_in_v[p], preferred_element_type=F32)
         d_send[p] = part[:, :C]
-        own[slot_of(p)] = part[:, C:]
+        own[chunk_of(p)] = part[:, C:]
         d_copy(p).start()
 
     def pair_sum(p):
         with jax.named_scope('pair_wait'):
             d_copy(p).wait_recv()
-        slot = slot_of(p)
-        own[slot] = own[slot] + d_recv[p]
-
-        @pl.when((slot < NA) & ((home == 1) | (slot >= NF)))
-        def _():
-            x_copy_of(slot, 0).start()
-
-        @pl.when((slot < NF) & (home == 0))
-        def _():
-            x_copy_of(slot, 2).start()
+        q = chunk_of(p)
+        own[q] = own[q] + d_recv[p]
+
+        @pl.when((q >= c0) & (q < a0))
+        def _():
+            c_copy(q - c0).start()
+
+        @pl.when((home == 1) & (q < c0))
+        def _():
+            x_copy_of(q, 0, 0).start()
+
+            @pl.when(q % 2 == 1)
+            def _():
+                x_copy_of(q - 1, 1, 0).start()
+
+        @pl.when((home == 0) & (q >= a0 + NF))
+        def _():
+            x_copy_of(q - a0, 0, a0).start()
+
+        @pl.when((home == 0) & (q >= a0) & (q < a0 + NF))
+        def _():
+            x_copy_of(q - a0, 2, a0).start()
 
     def up_step(p, _):
-        late = p // (2 * NB)
-        up(p, (1 - late) * pos_col(p) + late * col_a(p - NB))
+        up(p)
         w_out_copy(p).start()
 
         @pl.when(p >= 2)
         def _():
             pair_sum(p - 2)
+
+        @pl.when((p == N - 2) & (home == 1))
+        def _():
+            pass_c(0)
         return 0
 
     lax.fori_loop(0, N, up_step, 0)
     pair_sum(N - 2)
     pair_sum(N - 1)
 
-    first_b = NF * (1 - home)
-    for m in range(NB // 2):
-        x_copy_of(first_b + 2 * m, 1).start()
+    @pl.when(home == 0)
+    def _():
+        for j in range(NF, NA, 2):
+            x_copy_of(j, 1, a0).start()
 
     with jax.named_scope('w_out_wait'):
         pltpu.make_async_copy(w_out_v, w_out_v, w_out_sem).wait()
@@ -248,9 +264,9 @@
     def back_copy(j, part):
         return remote(part_of(hall, 2 * NA + j, part), part_of(hall, 2 * NA + j, part), b_ssem, b_sem(j, part), y_next)
 
-    def make_h(j, part):
+    def make_h(j, part, first):
         with jax.named_scope('x_wait'):
-            x_copy_of(j, part).wait_recv()
+            x_copy_of(j, part, 0).wait_recv()
         if part == 2:
             rows, chunks = pl.ds(0, rows_a + rows_b), (j,)
         elif part == 0:
@@ -258,9 +274,16 @@
         else:
             rows, chunks = row_group[1], (j, j + 1)
         for c in chunks:
-            total = own[NA + c, rows, :] + x_recv[c, rows, :]
+            total = own[first + c, rows, :] + x_recv[c, rows, :]
             hall[c, rows, :] = jax.nn.gelu(total, approximate=True).astype(BF16)
         y_copy(j, part).start()
+
+    def make_h_c(j):
+        with jax.named_scope('c_wait'):
+            c_copy(j).wait_recv()
+            c_relay(j).wait_recv()
+        hall[c0 + j] = jax.nn.gelu(c_recv[0, j] + c_recv[1, j], approximate=True).astype(BF16)
+        y_copy(c0 + j, 2).start()
 
     def down(slot, i, part):
         if part == 2:
@@ -323,43 +346,65 @@
                 back_copy(i, part).wait_recv()
             down(2 * NA + i, i, part)
 
+        def c_step(i):
+            with jax.named_scope('ch_wait'):
+                y_copy(c0 + i, 2).wait_recv()
+            down(NA + c0 + i, c0 + i, 2)
+
         def a_step(j, part):
-            make_h(j, part)
-            down(j, NB + j, part)
-
+            make_h(j, part, a0)
+            down(j, a0 + j, part)
+
+        pass_c(1)
         loop(0, NF, lambda j: a_step(j, 2))
 
+        def step(j):
+            for t, i in ((3, 2), (5, 3), (6, 4)):
+                @pl.when(j == t)
+                def _():
+                    pass_c(i)
+            a_step(j, 0)
+
+        loop(NF, 8, step)
+
         def step(t):
-            @pl.when((t >= 1) & (t < 5))
+            @pl.when(t < 2)
             def _():
-                relay(2 * t - 2, 0)
-                relay(2 * t - 1, 0)
-
-            @pl.when(t >= 5)
+                relay(2 * t, 0)
+                relay(2 * t + 1, 0)
+
+            @pl.when(t == 2)
             def _():
-                relay(2 * (t - 5), 1)
-            a_step(NF + t, 0)
-
-        loop(0, NA - NF, step)
-        relay(NB - 2, 1)
-
-        def step(m):
-            b_step(2 * m, 0)
-            a_step(NF + 2 * m, 1)
-            b_step(2 * m + 1, 0)
-
-        loop(0, NB // 2, step)
+                relay(0, 1)
+                relay(2, 1)
+            c_step(t)
+            a_step(8 + t, 0)
+
+        loop(0, 3, step)
+
+        def step(t):
+            a_step(NF + 2 * t, 1)
+            c_step(3 + t)
+
+        loop(0, 2, step)
+
+        def step(t):
+            a_step(NF + 4 + 2 * t, 1)
+            b_step(2 * t, 0)
+            b_step(2 * t + 1, 0)
+
+        loop(0, 2, step)
         end_start(0)
         loop(0, 1, lambda m: b_step(2 * m, 1))
         end_send(0)
-        loop(1, NB // 2, lambda m: b_step(2 * m, 1))
+        loop(1, 2, lambda m: b_step(2 * m, 1))
 
     @pl.when(home == 0)
     def _():
         def a_step(j, part):
             with jax.named_scope('a_wait'):
                 y_copy(j, part).wait_recv()
-            down(NA + j, NB + j, part)
+            down(NA + j, a0 + j, part)
 
         def b_step(i, part):
             with jax.named_scope('b_wait'):
@@ -367,35 +412,39 @@
             back_copy(i, part).start()
             down(2 * NA + i, i, part)
 
-        loop(0, NB, lambda j: make_h(j, 0))
+        def c_step(i):
+            make_h_c(i)
+            down(c0 + i, c0 + i, 2)
+
+        loop(0, NB, lambda j: make_h(j, 0, 0))
+        loop(0, NB // 2, lambda m: make_h(2 * m, 1, 0))
+        c_step(0)
+        a_step(0, 2)
+        c_step(1)
+        loop(1, NF, lambda j: a_step(j, 2))
 
         def step(t):
-            a_step(2 * t, 2)
-            a_step(2 * t + 1, 2)
-            make_h(2 * t, 1)
+            c_step(2 + t)
+            loop(NF + 3 * t, NF + 3 * t + 3, lambda j: a_step(j, 0))
 
         loop(0, 2, step)
-
-        def step(t):
-            a_step(NF + 2 * t, 0)
-            make_h(4 + 2 * t, 1)
-            a_step(NF + 2 * t + 1, 0)
-
-        loop(0, 2, step)
+        c_step(4)
 
         def step(t):
             b_step(2 * t, 0)
+            a_step(NF + 6 + t, 0)
             b_step(2 * t + 1, 0)
-            a_step(NF + 4 + t, 0)
-
-        loop(0, 4, step)
+
+        loop(0, 2, step)
         end_start(0)
-        loop(0, 2, lambda m: b_step(2 * m, 1))
-        end_send(0)
-
-        def step(m):
-            b_step(4 + 2 * m, 1)
-            a_step(NF + 2 * m, 1)
+
+        def step(t):
+            b_step(2 * t, 1)
+            a_step(NF + 2 * t, 1)
+
+            @pl.when(t == 0)
+            def _():
+                end_send(0)
 
         loop(0, 2, step)
         loop(2, 4, lambda m: a_step(NF + 2 * m, 1))
@@ -411,18 +460,20 @@
         sent(x_g, z_ssem)
         sent(d_send, d_ssem)
         sent(hall.at[pl.ds(0, NB)], b_ssem)
+        sent(c_recv.at[0], c_ssem)
         sent(ea_recv, e_ssem)
         sent(eb_recv, e_ssem)
 
         @pl.when(home == 0)
         def _():
             sent(own.at[pl.ds(0, NA)], x_ssem)
-            sent(hall.at[pl.ds(0, NB)], y_ssem)
+            sent(hall.at[pl.ds(0, NB + NC)], y_ssem)
 
         @pl.when(home == 1)
         def _():
             gain_cp.wait_send()
             sent(own.at[pl.ds(0, NB)], x_ssem)
+            sent(c_recv.at[1], c_ssem)
             sent(hall.at[pl.ds(0, NA)], y_ssem)
 
     end_sum(0)
@@ -453,8 +504,9 @@
                 pltpu.VMEM((N, C, half), BF16),
                 pltpu.VMEM((N, tokens, C), F32),
                 pltpu.VMEM((N, tokens, C), F32),
-                pltpu.VMEM((2 * NA, tokens, C), F32),
+                pltpu.VMEM((N, tokens, C), F32),
                 pltpu.VMEM((NA, tokens, C), F32),
+                pltpu.VMEM((2, NC, tokens, C), F32),
                 pltpu.VMEM((2 * NA + NB, tokens, C), BF16),
                 pltpu.VMEM((tokens, half), F32),
                 pltpu.VMEM((2, TA, half), F32),
@@ -465,11 +517,12 @@
                 pltpu.VMEM((tok - TA, half), F32),
                 dma((8,)),
                 dma((N // GROUP,)),
-                dma((8,)),
+                dma((9,)),
                 dma((RING,)),
                 dma((NA + NA // 2,)),
                 dma((NA + NA // 2,)),
                 dma((NB + NB // 2,)),
+                dma((2 * NC,)),
                 dma((4,)),
                 dma((2,)),
             ],

time: 48.7 us -> 49 us (level)
  no operation moved by 1% of the time
where the time goes in v4:
time: 49 us; the launch traced here: 48.9 us
  Pallas kernels  48.2 us (98%)
  local copies, waits for them, and re-layouts  0.65 us (1%)
    pallas_call x1, Pallas kernels, body(): pl.pallas_call(kernel, out_shape=pltpu.VMEM((tok, half), BF16), in_specs=...  48.2 us

profile of v4, /device:TPU:0, one launch (start us, length us, event | category | flops | bytes accessed | tf_op | source)
XLA Modules:
  0.0 48.9 jit_solution(16664398275887826489)
XLA Ops:
  0.0 48.2 %shard_map.46 = bf16[24,2560]{1,0:T(8,128)(2,1)S(1)} custom-call(bf16[24,2560]{1,0:T(8,128)(2,1)} %x_hbm.1, f32[2560]{0:T(1024)} %gain_hbm.1, bf16[1280,10240]{1,0:T(8,128)(2,1)} %w_in_hbm.1, bf16[5120,2560]{1,0:T(8,128)(2,1)} %w_out_hbm.1), custom_call_target="tpu_custom_call" | custom-call | tf_op jit(solution)/shard_map/pallas_call | solution.py:491
  48.3 0.7 %copy.6 = bf16[24,2560]{1,0:T(8,128)(2,1)} copy(bf16[24,2560]{1,0:T(8,128)(2,1)S(1)} %shard_map.46) | data formatting | bytes 245760

commit v5 on v4

--- a/solution.py
+++ b/solution.py
@@ -22,10 +22,10 @@
 
 
 def kernel(x_hbm, gain_hbm, w_in_hbm, w_out_hbm, out_v,
-           x_v, gain_v, stat_g, x_g, x_relay, z_v, w_in_v, w_out_v, d_send, d_recv, own, x_recv, c_recv, hall,
+           xa_v, xb_v, gain_v, stat_g, x_ga, x_gb, x_relay, z_v, w_in_v, w_out_v, d_send, d_recv, own, x_recv, c_recv, hall,
            acc, ea_recv, eb_recv, fa_send, fa_recv, fb_send, fb_recv,
            misc_sem, w_in_sem, send_sem, d_rsem, x_rsem, y_rsem, b_rsem, c_rsem, e_rsem, f_rsem):
-    w_out_sem, stat_rsem, z_rsem = misc_sem.at[4], misc_sem.at[5], misc_sem.at[6]
+    w_out_sem, stat_rsem, za_rsem, zb_rsem = [misc_sem.at[i] for i in range(4, 8)]
     stat_ssem, z_ssem, d_ssem, x_ssem, y_ssem, b_ssem, c_ssem, e_ssem, f_ssem = [send_sem.at[i] for i in range(9)]
     y = lax.axis_index("col")
     row = lax.axis_index("row")
@@ -33,7 +33,7 @@
     k = row % 2
     dp = lax.axis_index("dp")
     home = 1 - (x + y) % 2
-    tok, half = x_v.shape
+    tok, half = out_v.shape
     feat = half // 2
     block = N * C
     rows_a = 4 * TA
@@ -67,9 +67,11 @@
         r = pl.multiple_of(i * C, C)
         return pltpu.make_async_copy(w_out_hbm.at[pl.ds(r, C), :], w_out_v.at[i], w_out_sem)
 
-    x_copy = pltpu.make_async_copy(x_hbm, x_v, misc_sem.at[0])
+    xa_copy = pltpu.make_async_copy(x_hbm.at[pl.ds(0, TA)], xa_v, misc_sem.at[0])
+    xb_copy = pltpu.make_async_copy(x_hbm.at[pl.ds(TA, tb)], xb_v, misc_sem.at[8])
     g_copy = pltpu.make_async_copy(gain_hbm, gain_v.at[0], misc_sem.at[1])
-    x_copy.start()
+    xa_copy.start()
+    xb_copy.start()
     g_copy.start()
 
     barrier = pltpu.get_barrier_semaphore()
@@ -85,22 +87,25 @@
 
     lax.fori_loop(0, N, start_w_in, 0)
 
-    x_copy.wait()
+    xa_copy.wait()
+    xb_copy.wait()
     g_copy.wait()
-    x_f = x_v[...].astype(F32)
-    s1 = jnp.sum(x_f, axis=1, keepdims=True)
-    s2 = jnp.sum(x_f * x_f, axis=1, keepdims=True)
-    lane = lax.broadcasted_iota(jnp.int32, (tok, 128), 1)
+
+    def row_sums(ref):
+        v = ref[...].astype(F32)
+        lane = lax.broadcasted_iota(jnp.int32, (v.shape[0], 128), 1)
+        return jnp.where(lane == 0, jnp.sum(v, axis=1, keepdims=True), jnp.sum(v * v, axis=1, keepdims=True))
+
     me = 4 * y + row
-    stat_g[me, :, :tok] = jnp.transpose(jnp.where(lane == 0, s1, s2))[:8]
+    stat_g[me, :, :tok] = jnp.transpose(jnp.concatenate([row_sums(xa_v), row_sums(xb_v)], axis=0))[:8]
     with jax.named_scope('barrier'):
         pl.semaphore_wait(barrier, 7)
 
-    def tok_copy(dy, dk):
-        ty = (y + dy) % 2
+    def tok_copy(group, dy, dk):
         tk = (k + dk) % 2
         cols = pl.ds(pl.multiple_of(feat * tk, 128), feat)
-        return remote(x_v.at[:, cols], x_g.at[row], z_ssem, z_rsem, (dp, ty, 2 * y + tk))
+        src, dst, sem = ((xa_v, x_ga, za_rsem), (xb_v, x_gb, zb_rsem))[group]
+        return remote(src.at[:, cols], dst.at[row], z_ssem, sem, (dp, (y + dy) % 2, 2 * y + tk))
 
     def stat_copy(d):
         ty = (y + d // 4) % 2
@@ -108,31 +113,39 @@
         return remote(stat_g.at[me], stat_g.at[me], stat_ssem, stat_rsem, (dp, ty, tr))
 
     gain_cp = remote(gain_v.at[0], gain_v.at[1], misc_sem.at[2], misc_sem.at[3], y_next)
-    half_cols = pl.ds(pl.multiple_of(feat * (1 - k), 128), feat)
-    to_relay = remote(x_v.at[:, half_cols], x_relay, z_ssem, misc_sem.at[7], y_next)
-    from_relay = remote(x_relay, x_g.at[row], z_ssem, z_rsem, (dp, y, 2 * (1 - x) + 1 - k))
+    def to_relay(tk):
+        return remote(xb_v.at[:, pl.ds(feat * tk, feat)], x_relay.at[tk], z_ssem, misc_sem.at[9], y_next)
+
+    def from_relay(tk):
+        return remote(x_relay.at[tk], x_gb.at[row], z_ssem, zb_rsem, (dp, y, 2 * (1 - x) + tk))
 
     for d in range(1, 8):
         stat_copy(d).start()
 
     @pl.when(home == 0)
     def _():
-        to_relay.start()
-        tok_copy(1, 0).start()
-        tok_copy(0, 0).start()
-        tok_copy(0, 1).start()
+        to_relay(0).start()
+        to_relay(1).start()
+        tok_copy(0, 1, 0).start()
+        tok_copy(0, 1, 1).start()
+        for group in range(2):
+            tok_copy(group, 0, 0).start()
+            tok_copy(group, 0, 1).start()
 
     @pl.when(home == 1)
     def _():
         gain_cp.start()
-        tok_copy(0, 1).start()
-        tok_copy(1, 0).start()
-        tok_copy(1, 1).start()
-        x_g[row] = jnp.where(k == 0, x_v[:, :feat], x_v[:, feat:])
+        for group in range(2):
+            tok_copy(group, 0, 1).start()
+            tok_copy(group, 1, 0).start()
+            tok_copy(group, 1, 1).start()
+        x_ga[row] = jnp.where(k == 0, xa_v[:, :feat], xa_v[:, feat:])
+        x_gb[row] = jnp.where(k == 0, xb_v[:, :feat], xb_v[:, feat:])
         gain_v[1] = gain_v[0]
         with jax.named_scope('x_relay_wait'):
-            to_relay.wait_recv()
-        from_relay.start()
+            remote(x_relay, x_relay, z_ssem, misc_sem.at[9], y_next).wait_recv()
+        from_relay(0).start()
+        from_relay(1).start()
 
     @pl.when(home == 0)
     def _():
@@ -143,72 +156,82 @@
     with jax.named_scope('stat_wait'):
         remote(stat_g.at[pl.ds(0, 7)], stat_g.at[pl.ds(0, 7)], stat_ssem, stat_rsem, y_next).wait_recv()
 
-    @pl.when(home == 0)
-    def _():
-        with jax.named_scope('z_wait'):
-            remote(x_g, x_g, z_ssem, z_rsem, y_next).wait_recv()
-
-    @pl.when(home == 1)
-    def _():
-        with jax.named_scope('z_wait'):
-            remote(x_g.at[pl.ds(0, 3)], x_g.at[pl.ds(0, 3)], z_ssem, z_rsem, y_next).wait_recv()
-    for src in range(4):
-        st = jnp.transpose(stat_g[src] + stat_g[4 + src])[:tok] * (1.0 / (2 * half))
-        mean = st[:, 0:1]
-        var = st[:, 1:2] - mean * mean
-        z = (x_g[src].astype(F32) - mean) * lax.rsqrt(var + NORM_EPS) * gain
-        z = z.astype(BF16)
-        z_v[pl.ds(TA * src, TA), :] = z[:TA]
-        z_v[pl.ds(rows_a + tb * src, tb), :] = z[TA:]
-
-    def d_copy(p):
-        return remote(d_send.at[p], d_recv.at[p], d_ssem, d_rsem.at[p % RING], sibling)
+    def make_z(group):
+        ref, sem = ((x_ga, za_rsem), (x_gb, zb_rsem))[group]
+
+        @pl.when(home == 0)
+        def _():
+            with jax.named_scope('z_wait'):
+                remote(ref, ref, z_ssem, sem, y_next).wait_recv()
+
+        @pl.when(home == 1)
+        def _():
+            with jax.named_scope('z_wait'):
+                remote(ref.at[pl.ds(0, 3)], ref.at[pl.ds(0, 3)], z_ssem, sem, y_next).wait_recv()
+
+        t0, n, base = ((0, TA, 0), (TA, tb, rows_a))[group]
+        for src in range(4):
+            st = jnp.transpose(stat_g[src] + stat_g[4 + src])[t0:t0 + n] * (1.0 / (2 * half))
+            mean = st[:, 0:1]
+            var = st[:, 1:2] - mean * mean
+            z = (ref[src].astype(F32) - mean) * lax.rsqrt(var + NORM_EPS) * gain
+            z_v[pl.ds(base + n * src, n), :] = z.astype(BF16)
 
     row_group = (pl.ds(0, rows_a), pl.ds(rows_a, rows_b))
 
     def part_of(ref, j, part):
         if part == 2:
             return ref.at[j]
-        if part == 0:
-            return ref.at[j, row_group[0]]
-        return ref.at[pl.ds(j, 2), row_group[1]]
+        if part == 1:
+            return ref.at[pl.ds(j, 2), row_group[1]]
+        return ref.at[j, row_group[part // 3]]
+
+    def d_copy(p, part, seq):
+        return remote(part_of(d_send, p, part), part_of(d_recv, p, part), d_ssem, d_rsem.at[seq % RING], sibling)
 
     def x_copy_of(j, part, first):
         sem = x_rsem.at[NA + j // 2] if part == 1 else x_rsem.at[j]
         return remote(part_of(own, first + j, part), part_of(x_recv, j, part), x_ssem, sem, x_next)
 
-    def c_copy(j):
-        return remote(own.at[c0 + j], c_recv.at[0, j], c_ssem, c_rsem.at[j], y_next)
+    def c_copy(j, part):
+        return remote(part_of(own, c0 + j, part), part_of(c_recv.at[0], j, part), c_ssem, c_rsem.at[j], y_next)
 
     def c_relay(j):
         return remote(c_recv.at[0, j], c_recv.at[1, j], c_ssem, c_rsem.at[NC + j], x_next)
 
     def pass_c(j):
         with jax.named_scope('c_wait'):
-            c_copy(j).wait_recv()
+            c_copy(j, 2).wait_recv()
         c_relay(j).start()
 
-    def up(p):
-        @pl.when(p % GROUP == 0)
-        def _():
-            with jax.named_scope('w_in_wait'):
-                group = w_in_v.at[pl.ds(p, GROUP)]
-                pltpu.make_async_copy(group, group, w_in_sem.at[p // GROUP]).wait()
-
-        part = jnp.dot(z_v[...], w_in_v[p], preferred_element_type=F32)
-        d_send[p] = part[:, :C]
-        own[chunk_of(p)] = part[:, C:]
-        d_copy(p).start()
+    def rows_of(part):
+        return pl.ds(0, rows_a + rows_b) if part == 2 else row_group[part // 3]
+
+    def up(p, part, seq):
+        rows = rows_of(part)
+        sums = jnp.dot(z_v[rows, :], w_in_v[p], preferred_element_type=F32)
+        d_send[p, rows, :] = sums[:, :C]
+        own[chunk_of(p), rows, :] = sums[:, C:]
+        d_copy(p, part, seq).start()
+
+    def pair_add(p, part, seq):
+        with jax.named_scope('pair_wait'):
+            d_copy(p, part, seq).wait_recv()
+        q, rows = chunk_of(p), rows_of(part)
+        own[q, rows, :] = own[q, rows, :] + d_recv[p, rows, :]
+
+    def wait_w_in(p):
+        with jax.named_scope('w_in_wait'):
+            group = w_in_v.at[pl.ds(p, GROUP)]
+            pltpu.make_async_copy(group, group, w_in_sem.at[p // GROUP]).wait()
 
     def pair_sum(p):
-        with jax.named_scope('pair_wait'):
-            d_copy(p).wait_recv()
+        pair_add(p, 2, p + 2)
         q = chunk_of(p)
-        own[q] = own[q] + d_recv[p]
 
         @pl.when((q >= c0) & (q < a0))
         def _():
-            c_copy(q - c0).start()
+            c_copy(q - c0, 2).start()
 
         @pl.when((home == 1) & (q < c0))
         def _():
@@ -227,19 +250,55 @@
             x_copy_of(q - a0, 2, a0).start()
 
     def up_step(p, _):
-        up(p)
+        @pl.when(p % GROUP == 0)
+        def _():
+            wait_w_in(p)
+        up(p, 2, p + 2)
         w_out_copy(p).start()
 
-        @pl.when(p >= 2)
+        @pl.when(p >= 4)
         def _():
             pair_sum(p - 2)
+
+        @pl.when((p >= 2) & (p < 4))
+        def _():
+            pair_add(p - 2, 3, p)
+
+            @pl.when(p == 3)
+            def _():
+                c_copy(0, 3).start()
+
+            @pl.when((p == 2) & (home == 0))
+            def _():
+                x_copy_of(0, 3, a0).start()
 
         @pl.when((p == N - 2) & (home == 1))
         def _():
             pass_c(0)
         return 0
 
-    lax.fori_loop(0, N, up_step, 0)
+    make_z(0)
+    wait_w_in(0)
+    up(0, 0, 0)
+    up(1, 0, 1)
+    make_z(1)
+    up(0, 3, 2)
+    w_out_copy(0).start()
+    pair_add(0, 0, 0)
+
+    @pl.when(home == 1)
+    def _():
+        x_copy_of(0, 0, 0).start()
+
+    @pl.when(home == 0)
+    def _():
+        x_copy_of(0, 0, a0).start()
+
+    up(1, 3, 3)
+    w_out_copy(1).start()
+    pair_add(1, 0, 1)
+    c_copy(0, 0).start()
+    lax.fori_loop(2, N, up_step, 0)
     pair_sum(N - 2)
     pair_sum(N - 1)
 
@@ -280,7 +339,7 @@
 
     def make_h_c(j):
         with jax.named_scope('c_wait'):
-            c_copy(j).wait_recv()
+            c_copy(j, 2).wait_recv()
             c_relay(j).wait_recv()
         hall[c0 + j] = jax.nn.gelu(c_recv[0, j] + c_recv[1, j], approximate=True).astype(BF16)
         y_copy(c0 + j, 2).start()
@@ -326,7 +385,7 @@
             f_copy(group).wait_recv()
         total = acc[token_rows(group, row), :] + e_recv[group][1] + f_recv[group][...]
         t0, n = ((0, TA), (TA, tb))[group]
-        out_v[t0:t0 + n, :] = (x_v[t0:t0 + n, :].astype(F32) + total).astype(BF16)
+        out_v[t0:t0 + n, :] = ((xa_v, xb_v)[group][...].astype(F32) + total).astype(BF16)
 
     def loop(lo, hi, step):
         def body(i, _):
@@ -368,36 +427,31 @@
         loop(NF, 8, step)
 
         def step(t):
-            @pl.when(t < 2)
-            def _():
-                relay(2 * t, 0)
-                relay(2 * t + 1, 0)
-
-            @pl.when(t == 2)
+            relay(2 * t, 0)
+            relay(2 * t + 1, 0)
+
+            @pl.when(t == 1)
             def _():
                 relay(0, 1)
                 relay(2, 1)
-            c_step(t)
             a_step(8 + t, 0)
 
-        loop(0, 3, step)
-
-        def step(t):
-            a_step(NF + 2 * t, 1)
-            c_step(3 + t)
-
         loop(0, 2, step)
-
-        def step(t):
-            a_step(NF + 4 + 2 * t, 1)
-            b_step(2 * t, 0)
-            b_step(2 * t + 1, 0)
-
-        loop(0, 2, step)
+        c_step(0)
+        a_step(10, 0)
+        loop(1, 3, c_step)
+        a_step(NF, 1)
+        c_step(3)
+        a_step(NF + 2, 1)
+        make_h(NF + 4, 1, a0)
+        c_step(4)
+        loop(0, 2, lambda i: b_step(i, 0))
+        make_h(NF + 6, 1, a0)
+        loop(2, 4, lambda i: b_step(i, 0))
         end_start(0)
-        loop(0, 1, lambda m: b_step(2 * m, 1))
+        loop(2, 4, lambda m: down(NF + 2 * m, a0 + NF + 2 * m, 1))
         end_send(0)
-        loop(1, 2, lambda m: b_step(2 * m, 1))
+        loop(0, 2, lambda m: b_step(2 * m, 1))
 
     @pl.when(home == 0)
     def _():
@@ -457,7 +511,6 @@
 
     with jax.named_scope('drain'):
         sent(stat_g.at[pl.ds(0, 7)], stat_ssem)
-        sent(x_g, z_ssem)
         sent(d_send, d_ssem)
         sent(hall.at[pl.ds(0, NB)], b_ssem)
         sent(c_recv.at[0], c_ssem)
@@ -466,12 +519,17 @@
 
         @pl.when(home == 0)
         def _():
+            sent(x_ga, z_ssem)
+            sent(x_gb, z_ssem)
             sent(own.at[pl.ds(0, NA)], x_ssem)
             sent(hall.at[pl.ds(0, NB + NC)], y_ssem)
 
         @pl.when(home == 1)
         def _():
             gain_cp.wait_send()
+            sent(x_ga.at[pl.ds(0, 3)], z_ssem)
+            sent(x_gb, z_ssem)
+            sent(x_gb.at[0], z_ssem)
             sent(own.at[pl.ds(0, NB)], x_ssem)
             sent(c_recv.at[1], c_ssem)
             sent(hall.at[pl.ds(0, NA)], y_ssem)
@@ -494,11 +552,13 @@
             in_specs=[pl.BlockSpec(memory_space=pl.ANY)] * 4,
             out_specs=pl.BlockSpec(memory_space=pltpu.VMEM),
             scratch_shapes=[
-                pltpu.VMEM((tok, half), BF16),
+                pltpu.VMEM((TA, half), BF16),
+                pltpu.VMEM((tok - TA, half), BF16),
                 pltpu.VMEM((2, half), F32),
                 pltpu.VMEM((8, 8, 128), F32),
-                pltpu.VMEM((4, tok, feat), BF16),
-                pltpu.VMEM((tok, feat), BF16),
+                pltpu.VMEM((4, TA, feat), BF16),
+                pltpu.VMEM((4, tok - TA, feat), BF16),
+                pltpu.VMEM((2, tok - TA, feat), BF16),
                 pltpu.VMEM((tokens, feat), BF16),
                 pltpu.VMEM((N, feat, 2 * C), BF16),
                 pltpu.VMEM((N, C, half), BF16),
@@ -515,7 +575,7 @@
                 pltpu.VMEM((TA, half), F32),
                 pltpu.VMEM((tok - TA, half), F32),
                 pltpu.VMEM((tok - TA, half), F32),
-                dma((8,)),
+                dma((10,)),
                 dma((N // GROUP,)),
                 dma((9,)),
                 dma((RING,)),

time: 49 us -> 48.1 us (0.982)
  Pallas kernels: 48.2 us -> 47.3 us
    pallas_call x1, Pallas kernels: 48.2 us -> 47.3 us  [body(): pl.pallas_call(kernel, out_shape=pltpu.VMEM((tok, half), BF16), in_specs=...]
where the time goes in v5:
time: 48.1 us; the launch traced here: 48 us
  Pallas kernels  47.3 us (98%)
  local copies, waits for them, and re-layouts  0.65 us (1%)
    pallas_call x1, Pallas kernels, body(): pl.pallas_call(kernel, out_shape=pltpu.VMEM((tok, half), BF16), in_specs=...  47.3 us

profile of v5, /device:TPU:0, one launch (start us, length us, event | category | flops | bytes accessed | tf_op | source)
XLA Modules:
  0.0 48.0 jit_solution(3648066767395009952)
XLA Ops:
  0.0 47.3 %shard_map.46 = bf16[24,2560]{1,0:T(8,128)(2,1)S(1)} custom-call(bf16[24,2560]{1,0:T(8,128)(2,1)} %x_hbm.1, f32[2560]{0:T(1024)} %gain_hbm.1, bf16[1280,10240]{1,0:T(8,128)(2,1)} %w_in_hbm.1, bf16[5120,2560]{1,0:T(8,128)(2,1)} %w_out_hbm.1), custom_call_target="tpu_custom_call" | custom-call | tf_op jit(solution)/shard_map/pallas_call | solution.py:549
  47.3 0.7 %copy.6 = bf16[24,2560]{1,0:T(8,128)(2,1)} copy(bf16[24,2560]{1,0:T(8,128)(2,1)S(1)} %shard_map.46) | data formatting | bytes 245760

commit v6 on v5

--- a/solution.py
+++ b/solution.py
@@ -7,6 +7,7 @@
 
 NORM_EPS = 1e-5
 MESH = pl.DeviceIdType.MESH
+WHOLE, FIRST = -1, 0
 F32 = jnp.float32
 BF16 = jnp.bfloat16
 
@@ -180,180 +181,144 @@
     row_group = (pl.ds(0, rows_a), pl.ds(rows_a, rows_b))
 
     def part_of(ref, j, part):
-        if part == 2:
+        if part == WHOLE:
             return ref.at[j]
-        if part == 1:
-            return ref.at[pl.ds(j, 2), row_group[1]]
-        return ref.at[j, row_group[part // 3]]
-
-    def d_copy(p, part, seq):
-        return remote(part_of(d_send, p, part), part_of(d_recv, p, part), d_ssem, d_rsem.at[seq % RING], sibling)
+        if part == FIRST:
+            return ref.at[j, row_group[0]]
+        return ref.at[pl.ds(j, part), row_group[1]]
+
+    def d_copy(p):
+        return remote(d_send.at[p], d_recv.at[p], d_ssem, d_rsem.at[p % RING], sibling)
 
     def x_copy_of(j, part, first):
-        sem = x_rsem.at[NA + j // 2] if part == 1 else x_rsem.at[j]
+        sem = x_rsem.at[NA + j // 2] if part > 0 else x_rsem.at[j]
         return remote(part_of(own, first + j, part), part_of(x_recv, j, part), x_ssem, sem, x_next)
 
-    def c_copy(j, part):
-        return remote(part_of(own, c0 + j, part), part_of(c_recv.at[0], j, part), c_ssem, c_rsem.at[j], y_next)
-
-    def c_relay(j):
-        return remote(c_recv.at[0, j], c_recv.at[1, j], c_ssem, c_rsem.at[NC + j], x_next)
+    def c_copy(j):
+        return remote(own.at[c0 + j], c_recv.at[0, j], c_ssem, c_rsem.at[j], y_next)
+
+    def c_relay(j, part):
+        sem = c_rsem.at[2 * NC + j // 3] if part > 0 else c_rsem.at[NC + j]
+        return remote(part_of(c_recv.at[0], j, part), part_of(c_recv.at[1], j, part), c_ssem, sem, x_next)
 
     def pass_c(j):
         with jax.named_scope('c_wait'):
-            c_copy(j, 2).wait_recv()
-        c_relay(j).start()
-
-    def rows_of(part):
-        return pl.ds(0, rows_a + rows_b) if part == 2 else row_group[part // 3]
-
-    def up(p, part, seq):
-        rows = rows_of(part)
-        sums = jnp.dot(z_v[rows, :], w_in_v[p], preferred_element_type=F32)
-        d_send[p, rows, :] = sums[:, :C]
-        own[chunk_of(p), rows, :] = sums[:, C:]
-        d_copy(p, part, seq).start()
-
-    def pair_add(p, part, seq):
+            c_copy(j).wait_recv()
+        c_relay(j, FIRST).start()
+
+    def up(p):
+        sums = jnp.dot(z_v[...], w_in_v[p], preferred_element_type=F32)
+        d_send[p] = sums[:, :C]
+        own[chunk_of(p)] = sums[:, C:]
+        d_copy(p).start()
+
+    def pair_sum(p):
         with jax.named_scope('pair_wait'):
-            d_copy(p, part, seq).wait_recv()
-        q, rows = chunk_of(p), rows_of(part)
-        own[q, rows, :] = own[q, rows, :] + d_recv[p, rows, :]
-
-    def wait_w_in(p):
-        with jax.named_scope('w_in_wait'):
-            group = w_in_v.at[pl.ds(p, GROUP)]
-            pltpu.make_async_copy(group, group, w_in_sem.at[p // GROUP]).wait()
-
-    def pair_sum(p):
-        pair_add(p, 2, p + 2)
+            d_copy(p).wait_recv()
         q = chunk_of(p)
+        own[q] = own[q] + d_recv[p]
 
         @pl.when((q >= c0) & (q < a0))
         def _():
-            c_copy(q - c0, 2).start()
+            c_copy(q - c0).start()
 
         @pl.when((home == 1) & (q < c0))
         def _():
-            x_copy_of(q, 0, 0).start()
+            x_copy_of(q, FIRST, 0).start()
 
             @pl.when(q % 2 == 1)
             def _():
-                x_copy_of(q - 1, 1, 0).start()
+                x_copy_of(q - 1, 2, 0).start()
 
         @pl.when((home == 0) & (q >= a0 + NF))
         def _():
-            x_copy_of(q - a0, 0, a0).start()
+            x_copy_of(q - a0, FIRST, a0).start()
 
         @pl.when((home == 0) & (q >= a0) & (q < a0 + NF))
         def _():
-            x_copy_of(q - a0, 2, a0).start()
+            x_copy_of(q - a0, WHOLE, a0).start()
 
     def up_step(p, _):
         @pl.when(p % GROUP == 0)
         def _():
-            wait_w_in(p)
-        up(p, 2, p + 2)
+            with jax.named_scope('w_in_wait'):
+                group = w_in_v.at[pl.ds(p, GROUP)]
+                pltpu.make_async_copy(group, group, w_in_sem.at[p // GROUP]).wait()
+        up(p)
         w_out_copy(p).start()
 
-        @pl.when(p >= 4)
+        @pl.when(p >= 2)
         def _():
             pair_sum(p - 2)
 
-        @pl.when((p >= 2) & (p < 4))
-        def _():
-            pair_add(p - 2, 3, p)
-
-            @pl.when(p == 3)
-            def _():
-                c_copy(0, 3).start()
-
-            @pl.when((p == 2) & (home == 0))
-            def _():
-                x_copy_of(0, 3, a0).start()
-
-        @pl.when((p == N - 2) & (home == 1))
+        @pl.when((p == 13) & (home == 1))
         def _():
             pass_c(0)
+
+        @pl.when((p == 18) & (home == 1))
+        def _():
+            pass_c(1)
         return 0
 
     make_z(0)
-    wait_w_in(0)
-    up(0, 0, 0)
-    up(1, 0, 1)
     make_z(1)
-    up(0, 3, 2)
-    w_out_copy(0).start()
-    pair_add(0, 0, 0)
-
-    @pl.when(home == 1)
-    def _():
-        x_copy_of(0, 0, 0).start()
-
-    @pl.when(home == 0)
-    def _():
-        x_copy_of(0, 0, a0).start()
-
-    up(1, 3, 3)
-    w_out_copy(1).start()
-    pair_add(1, 0, 1)
-    c_copy(0, 0).start()
-    lax.fori_loop(2, N, up_step, 0)
+    lax.fori_loop(0, N, up_step, 0)
     pair_sum(N - 2)
     pair_sum(N - 1)
 
     @pl.when(home == 0)
     def _():
         for j in range(NF, NA, 2):
-            x_copy_of(j, 1, a0).start()
+            x_copy_of(j, 2, a0).start()
 
     with jax.named_scope('w_out_wait'):
         pltpu.make_async_copy(w_out_v, w_out_v, w_out_sem).wait()
 
     def y_copy(j, part):
-        sem = y_rsem.at[NA + j // 2] if part == 1 else y_rsem.at[j]
+        sem = y_rsem.at[NA + j // 2] if part > 0 else y_rsem.at[j]
         return remote(part_of(hall, j, part), part_of(hall, NA + j, part), y_ssem, sem, y_next)
 
     def b_sem(j, part):
-        return b_rsem.at[NB + j // 2] if part == 1 else b_rsem.at[j]
+        return b_rsem.at[NB + j // 2] if part > 0 else b_rsem.at[j]
 
     def relay_copy(j, part):
         return remote(part_of(hall, NA + j, part), part_of(hall, 2 * NA + j, part), b_ssem, b_sem(j, part), x_next)
 
     def back_copy(j, part):
         return remote(part_of(hall, 2 * NA + j, part), part_of(hall, 2 * NA + j, part), b_ssem, b_sem(j, part), y_next)
+
+    def rows_of(part):
+        return pl.ds(0, rows_a + rows_b) if part == WHOLE else row_group[int(part > 0)]
+
+    def put_h(j, part, left, right):
+        rows = rows_of(part)
+        for c in range(max(part, 1)):
+            total = left(c)[rows, :] + right(c)[rows, :]
+            hall[j + c, rows, :] = jax.nn.gelu(total, approximate=True).astype(BF16)
 
     def make_h(j, part, first):
         with jax.named_scope('x_wait'):
             x_copy_of(j, part, 0).wait_recv()
-        if part == 2:
-            rows, chunks = pl.ds(0, rows_a + rows_b), (j,)
-        elif part == 0:
-            rows, chunks = row_group[0], (j,)
-        else:
-            rows, chunks = row_group[1], (j, j + 1)
-        for c in chunks:
-            total = own[first + c, rows, :] + x_recv[c, rows, :]
-            hall[c, rows, :] = jax.nn.gelu(total, approximate=True).astype(BF16)
+        put_h(j, part, lambda c: own.at[first + j + c], lambda c: x_recv.at[j + c])
         y_copy(j, part).start()
 
-    def make_h_c(j):
+    def make_h_c(j, part):
         with jax.named_scope('c_wait'):
-            c_copy(j, 2).wait_recv()
-            c_relay(j).wait_recv()
-        hall[c0 + j] = jax.nn.gelu(c_recv[0, j] + c_recv[1, j], approximate=True).astype(BF16)
-        y_copy(c0 + j, 2).start()
+            if part == FIRST:
+                c_copy(j).wait_recv()
+            c_relay(j, part).wait_recv()
+        put_h(c0 + j, part, lambda c: c_recv.at[0, j + c], lambda c: c_recv.at[1, j + c])
+        yc_copy(j, part).start()
+
+    def yc_copy(j, part):
+        sem = y_rsem.at[NA + 2 + j // 3] if part > 0 else y_rsem.at[c0 + j]
+        return remote(part_of(hall, c0 + j, part), part_of(hall, NA + c0 + j, part), y_ssem, sem, y_next)
 
     def down(slot, i, part):
-        if part == 2:
-            acc[...] += jnp.dot(hall[slot], w_out_v[i], preferred_element_type=F32)
-        elif part == 0:
-            rows = row_group[0]
-            acc[rows, :] += jnp.dot(hall[slot, rows, :], w_out_v[i], preferred_element_type=F32)
-        else:
-            rows = row_group[1]
-            acc[rows, :] += (jnp.dot(hall[slot, rows, :], w_out_v[i], preferred_element_type=F32)
-                             + jnp.dot(hall[slot + 1, rows, :], w_out_v[i + 1], preferred_element_type=F32))
+        rows = rows_of(part)
+        parts = [jnp.dot(hall[slot + c, rows, :], w_out_v[i + c], preferred_element_type=F32)
+                 for c in range(max(part, 1))]
+        acc[rows, :] += sum(parts[1:], parts[0])
 
     e_recv, f_send, f_recv = (ea_recv, eb_recv), (fa_send, fb_send), (fa_recv, fb_recv)
 
@@ -405,53 +370,61 @@
                 back_copy(i, part).wait_recv()
             down(2 * NA + i, i, part)
 
-        def c_step(i):
+        def c_step(i, part):
             with jax.named_scope('ch_wait'):
-                y_copy(c0 + i, 2).wait_recv()
-            down(NA + c0 + i, c0 + i, 2)
+                yc_copy(i, part).wait_recv()
+            down(NA + c0 + i, c0 + i, part)
 
         def a_step(j, part):
             make_h(j, part, a0)
             down(j, a0 + j, part)
 
-        pass_c(1)
-        loop(0, NF, lambda j: a_step(j, 2))
+        loop(0, NF, lambda j: a_step(j, WHOLE))
 
         def step(j):
-            for t, i in ((3, 2), (5, 3), (6, 4)):
+            for t, i in ((3, 2), (4, 3), (6, 4)):
                 @pl.when(j == t)
                 def _():
                     pass_c(i)
-            a_step(j, 0)
-
-        loop(NF, 8, step)
+
+            @pl.when(j == 7)
+            def _():
+                relay(0, FIRST)
+                relay(1, FIRST)
+
+            @pl.when(j == 8)
+            def _():
+                relay(2, FIRST)
+                relay(3, FIRST)
+                c_relay(0, 3).start()
+                c_relay(3, 2).start()
+                relay(0, 2)
+                relay(2, 2)
+            a_step(j, FIRST)
+
+        loop(NF, 9, step)
 
         def step(t):
-            relay(2 * t, 0)
-            relay(2 * t + 1, 0)
-
-            @pl.when(t == 1)
-            def _():
-                relay(0, 1)
-                relay(2, 1)
-            a_step(8 + t, 0)
+            c_step(2 * t, FIRST)
+            a_step(9 + t, FIRST)
+            c_step(2 * t + 1, FIRST)
 
         loop(0, 2, step)
-        c_step(0)
-        a_step(10, 0)
-        loop(1, 3, c_step)
-        a_step(NF, 1)
-        c_step(3)
-        a_step(NF + 2, 1)
-        make_h(NF + 4, 1, a0)
-        c_step(4)
-        loop(0, 2, lambda i: b_step(i, 0))
-        make_h(NF + 6, 1, a0)
-        loop(2, 4, lambda i: b_step(i, 0))
+        c_step(4, FIRST)
+
+        def step(t):
+            a_step(NF + 2 * t, 2)
+            b_step(2 * t, FIRST)
+            b_step(2 * t + 1, FIRST)
+
+        loop(0, 2, step)
         end_start(0)
-        loop(2, 4, lambda m: down(NF + 2 * m, a0 + NF + 2 * m, 1))
+        a_step(NF + 4, 2)
         end_send(0)
-        loop(0, 2, lambda m: b_step(2 * m, 1))
+        a_step(NF + 6, 2)
+        c_step(0, 3)
+        c_step(3, 2)
+        loop(0, 2, lambda m: b_step(2 * m, 2))
 
     @pl.when(home == 0)
     def _():
@@ -466,42 +439,39 @@
             back_copy(i, part).start()
             down(2 * NA + i, i, part)
 
-        def c_step(i):
-            make_h_c(i)
-            down(c0 + i, c0 + i, 2)
-
-        loop(0, NB, lambda j: make_h(j, 0, 0))
-        loop(0, NB // 2, lambda m: make_h(2 * m, 1, 0))
-        c_step(0)
-        a_step(0, 2)
-        c_step(1)
-        loop(1, NF, lambda j: a_step(j, 2))
+        def c_step(i, part):
+            make_h_c(i, part)
+            down(c0 + i, c0 + i, part)
+
+        loop(0, NB, lambda j: make_h(j, FIRST, 0))
+        loop(0, NB // 2, lambda m: make_h(2 * m, 2, 0))
+        c_step(0, FIRST)
 
         def step(t):
-            c_step(2 + t)
-            loop(NF + 3 * t, NF + 3 * t + 3, lambda j: a_step(j, 0))
+            c_step(1 + t, FIRST)
+            a_step(t, WHOLE)
+
+        loop(0, NF, step)
+        a_step(NF, FIRST)
+        c_step(4, FIRST)
+
+        def step(t):
+            a_step(NF + 1 + t, FIRST)
+            b_step(t, FIRST)
+
+        loop(0, 4, step)
+        loop(NF + 5, NA, lambda j: a_step(j, FIRST))
+        end_start(0)
+        c_step(0, 3)
+        end_send(0)
+        c_step(3, 2)
+
+        def step(t):
+            b_step(2 * t, 2)
+            a_step(NF + 2 * t, 2)
 
         loop(0, 2, step)
-        c_step(4)
-
-        def step(t):
-            b_step(2 * t, 0)
-            a_step(NF + 6 + t, 0)
-            b_step(2 * t + 1, 0)
-
-        loop(0, 2, step)
-        end_start(0)
-
-        def step(t):
-            b_step(2 * t, 1)
-            a_step(NF + 2 * t, 1)
-
-            @pl.when(t == 0)
-            def _():
-                end_send(0)
-
-        loop(0, 2, step)
-        loop(2, 4, lambda m: a_step(NF + 2 * m, 1))
+        loop(2, 4, lambda m: a_step(NF + 2 * m, 2))
 
     end_start(1)
     end_send(1)
@@ -582,7 +552,7 @@
                 dma((NA + NA // 2,)),
                 dma((NA + NA // 2,)),
                 dma((NB + NB // 2,)),
-                dma((2 * NC,)),
+                dma((2 * NC + 2,)),
                 dma((4,)),
                 dma((2,)),
             ],

time: 48.1 us -> 47.5 us (0.988)
  Pallas kernels: 47.3 us -> 46.8 us
    pallas_call x1, Pallas kernels: 47.3 us -> 46.8 us  [body(): pl.pallas_call(kernel, out_shape=pltpu.VMEM((tok, half), BF16), in_specs=...]
where the time goes in v6:
time: 47.5 us; the launch traced here: 47.4 us
  Pallas kernels  46.8 us (99%)
  local copies, waits for them, and re-layouts  0.65 us (1%)
    pallas_call x1, Pallas kernels, body(): pl.pallas_call(kernel, out_shape=pltpu.VMEM((tok, half), BF16), in_specs=...  46.8 us

profile of v6, /device:TPU:0, one launch (start us, length us, event | category | flops | bytes accessed | tf_op | source)
XLA Modules:
  0.0 47.4 jit_solution(15328497517013675179)
XLA Ops:
  0.0 46.8 %shard_map.46 = bf16[24,2560]{1,0:T(8,128)(2,1)S(1)} custom-call(bf16[24,2560]{1,0:T(8,128)(2,1)} %x_hbm.1, f32[2560]{0:T(1024)} %gain_hbm.1, bf16[1280,10240]{1,0:T(8,128)(2,1)} %w_in_hbm.1, bf16[5120,2560]{1,0:T(8,128)(2,1)} %w_out_hbm.1), custom_call_target="tpu_custom_call" | custom-call | tf_op jit(solution)/shard_map/pallas_call | solution.py:519
  46.8 0.7 %copy.6 = bf16[24,2560]{1,0:T(8,128)(2,1)} copy(bf16[24,2560]{1,0:T(8,128)(2,1)S(1)} %shard_map.46) | data formatting | bytes 245760

commit v7 on v6

--- a/solution.py
+++ b/solution.py
@@ -98,7 +98,6 @@
         return jnp.where(lane == 0, jnp.sum(v, axis=1, keepdims=True), jnp.sum(v * v, axis=1, keepdims=True))
 
     me = 4 * y + row
-    stat_g[me, :, :tok] = jnp.transpose(jnp.concatenate([row_sums(xa_v), row_sums(xb_v)], axis=0))[:8]
     with jax.named_scope('barrier'):
         pl.semaphore_wait(barrier, 7)
 
@@ -120,14 +119,24 @@
     def from_relay(tk):
         return remote(x_relay.at[tk], x_gb.at[row], z_ssem, zb_rsem, (dp, y, 2 * (1 - x) + tk))
 
-    for d in range(1, 8):
-        stat_copy(d).start()
-
     @pl.when(home == 0)
     def _():
         to_relay(0).start()
         to_relay(1).start()
         tok_copy(0, 1, 0).start()
+
+    @pl.when(home == 1)
+    def _():
+        gain_cp.start()
+        tok_copy(0, 0, 1).start()
+        tok_copy(0, 1, 0).start()
+
+    stat_g[me, :, :tok] = jnp.transpose(jnp.concatenate([row_sums(xa_v), row_sums(xb_v)], axis=0))[:8]
+    for d in range(1, 8):
+        stat_copy(d).start()
+
+    @pl.when(home == 0)
+    def _():
         tok_copy(0, 1, 1).start()
         for group in range(2):
             tok_copy(group, 0, 0).start()
@@ -135,11 +144,10 @@
 
     @pl.when(home == 1)
     def _():
-        gain_cp.start()
-        for group in range(2):
-            tok_copy(group, 0, 1).start()
-            tok_copy(group, 1, 0).start()
-            tok_copy(group, 1, 1).start()
+        tok_copy(0, 1, 1).start()
+        tok_copy(1, 0, 1).start()
+        tok_copy(1, 1, 0).start()
+        tok_copy(1, 1, 1).start()
         x_ga[row] = jnp.where(k == 0, xa_v[:, :feat], xa_v[:, feat:])
         x_gb[row] = jnp.where(k == 0, xb_v[:, :feat], xb_v[:, feat:])
         gain_v[1] = gain_v[0]
@@ -187,15 +195,21 @@
             return ref.at[j, row_group[0]]
         return ref.at[pl.ds(j, part), row_group[1]]
 
-    def d_copy(p):
-        return remote(d_send.at[p], d_recv.at[p], d_ssem, d_rsem.at[p % RING], sibling)
+    def rows_of(part):
+        return pl.ds(0, rows_a + rows_b) if part == WHOLE else row_group[int(part > 0)]
+
+    def d_copy(p, part, seq):
+        return remote(part_of(d_send, p, part), part_of(d_recv, p, part), d_ssem, d_rsem.at[seq % RING], sibling)
 
     def x_copy_of(j, part, first):
         sem = x_rsem.at[NA + j // 2] if part > 0 else x_rsem.at[j]
         return remote(part_of(own, first + j, part), part_of(x_recv, j, part), x_ssem, sem, x_next)
 
     def c_copy(j):
-        return remote(own.at[c0 + j], c_recv.at[0, j], c_ssem, c_rsem.at[j], y_next)
+        return c_part(j, WHOLE)
+
+    def c_part(j, part):
+        return remote(part_of(own, c0 + j, part), part_of(c_recv.at[0], j, part), c_ssem, c_rsem.at[j], y_next)
 
     def c_relay(j, part):
         sem = c_rsem.at[2 * NC + j // 3] if part > 0 else c_rsem.at[NC + j]
@@ -206,17 +220,27 @@
             c_copy(j).wait_recv()
         c_relay(j, FIRST).start()
 
-    def up(p):
-        sums = jnp.dot(z_v[...], w_in_v[p], preferred_element_type=F32)
-        d_send[p] = sums[:, :C]
-        own[chunk_of(p)] = sums[:, C:]
-        d_copy(p).start()
+    def up(p, part, seq):
+        rows = rows_of(part)
+        sums = jnp.dot(z_v[rows, :], w_in_v[p], preferred_element_type=F32)
+        d_send[p, rows, :] = sums[:, :C]
+        own[chunk_of(p), rows, :] = sums[:, C:]
+        d_copy(p, part, seq).start()
+
+    def pair_add(p, part, seq):
+        with jax.named_scope('pair_wait'):
+            d_copy(p, part, seq).wait_recv()
+        q, rows = chunk_of(p), rows_of(part)
+        own[q, rows, :] = own[q, rows, :] + d_recv[p, rows, :]
+
+    def wait_w_in(p):
+        with jax.named_scope('w_in_wait'):
+            group = w_in_v.at[pl.ds(p, GROUP)]
+            pltpu.make_async_copy(group, group, w_in_sem.at[p // GROUP]).wait()
 
     def pair_sum(p):
-        with jax.named_scope('pair_wait'):
-            d_copy(p).wait_recv()
+        pair_add(p, WHOLE, p + 2)
         q = chunk_of(p)
-        own[q] = own[q] + d_recv[p]
 
         @pl.when((q >= c0) & (q < a0))
         def _():
@@ -241,15 +265,25 @@
     def up_step(p, _):
         @pl.when(p % GROUP == 0)
         def _():
-            with jax.named_scope('w_in_wait'):
-                group = w_in_v.at[pl.ds(p, GROUP)]
-                pltpu.make_async_copy(group, group, w_in_sem.at[p // GROUP]).wait()
-        up(p)
+            wait_w_in(p)
+        up(p, WHOLE, p + 2)
         w_out_copy(p).start()
 
-        @pl.when(p >= 2)
+        @pl.when(p >= 4)
         def _():
             pair_sum(p - 2)
+
+        @pl.when((p >= 2) & (p < 4))
+        def _():
+            pair_add(p - 2, 1, p)
+
+            @pl.when(p == 3)
+            def _():
+                c_part(0, 1).start()
+
+            @pl.when((p == 2) & (home == 0))
+            def _():
+                first_b_part().start()
 
         @pl.when((p == 13) & (home == 1))
         def _():
@@ -260,16 +294,40 @@
             pass_c(1)
         return 0
 
+    def first_b_part():
+        return remote(part_of(own, a0, 1), part_of(x_recv, 0, 1), x_ssem, x_rsem.at[0], x_next)
+
     make_z(0)
+    wait_w_in(0)
+    up(0, FIRST, 0)
+    up(1, FIRST, 1)
     make_z(1)
-    lax.fori_loop(0, N, up_step, 0)
+    up(0, 1, 2)
+    w_out_copy(0).start()
+    pair_add(0, FIRST, 0)
+
+    @pl.when(home == 1)
+    def _():
+        x_copy_of(0, FIRST, 0).start()
+
+    @pl.when(home == 0)
+    def _():
+        x_copy_of(0, FIRST, a0).start()
+
+    up(1, 1, 3)
+    w_out_copy(1).start()
+    pair_add(1, FIRST, 1)
+    c_part(0, FIRST).start()
+    lax.fori_loop(2, N, up_step, 0)
     pair_sum(N - 2)
     pair_sum(N - 1)
 
     @pl.when(home == 0)
     def _():
-        for j in range(NF, NA, 2):
+        for j in range(NF, NA - 2, 2):
             x_copy_of(j, 2, a0).start()
+        x_copy_of(NA - 2, 1, a0).start()
+        x_copy_of(NA - 1, 1, a0).start()
 
     with jax.named_scope('w_out_wait'):
         pltpu.make_async_copy(w_out_v, w_out_v, w_out_sem).wait()
@@ -286,9 +344,6 @@
 
     def back_copy(j, part):
         return remote(part_of(hall, 2 * NA + j, part), part_of(hall, 2 * NA + j, part), b_ssem, b_sem(j, part), y_next)
-
-    def rows_of(part):
-        return pl.ds(0, rows_a + rows_b) if part == WHOLE else row_group[int(part > 0)]
 
     def put_h(j, part, left, right):
         rows = rows_of(part)
@@ -387,41 +442,38 @@
                 def _():
                     pass_c(i)
 
-            @pl.when(j == 7)
+            @pl.when(j == 8)
             def _():
                 relay(0, FIRST)
                 relay(1, FIRST)
-
-            @pl.when(j == 8)
+            a_step(j, FIRST)
+
+        loop(NF, 9, step)
+        relay(2, FIRST)
+        relay(3, FIRST)
+        c_relay(0, 3).start()
+        c_relay(3, 2).start()
+
+        def step(t):
+            a_step(9 + t, FIRST)
+
+            @pl.when(t == 0)
             def _():
-                relay(2, FIRST)
-                relay(3, FIRST)
-                c_relay(0, 3).start()
-                c_relay(3, 2).start()
                 relay(0, 2)
                 relay(2, 2)
-            a_step(j, FIRST)
-
-        loop(NF, 9, step)
-
-        def step(t):
             c_step(2 * t, FIRST)
-            a_step(9 + t, FIRST)
             c_step(2 * t + 1, FIRST)
 
         loop(0, 2, step)
+        a_step(NF, 2)
         c_step(4, FIRST)
-
-        def step(t):
-            a_step(NF + 2 * t, 2)
-            b_step(2 * t, FIRST)
-            b_step(2 * t + 1, FIRST)
-
-        loop(0, 2, step)
+        b_step(0, FIRST)
+        a_step(NF + 2, 2)
+        loop(1, NB, lambda i: b_step(i, FIRST))
         end_start(0)
         a_step(NF + 4, 2)
         end_send(0)
-        a_step(NF + 6, 2)
+        loop(NA - 2, NA, lambda j: a_step(j, 1))
         c_step(0, 3)
         c_step(3, 2)
         loop(0, 2, lambda m: b_step(2 * m, 2))
@@ -463,15 +515,13 @@
         loop(NF + 5, NA, lambda j: a_step(j, FIRST))
         end_start(0)
         c_step(0, 3)
+        c_step(3, 2)
+        b_step(0, 2)
         end_send(0)
-        c_step(3, 2)
-
-        def step(t):
-            b_step(2 * t, 2)
-            a_step(NF + 2 * t, 2)
-
-        loop(0, 2, step)
-        loop(2, 4, lambda m: a_step(NF + 2 * m, 2))
+        a_step(NF, 2)
+        b_step(2, 2)
+        loop(1, 3, lambda m: a_step(NF + 2 * m, 2))
+        loop(NA - 2, NA, lambda j: a_step(j, 1))
 
     end_start(1)
     end_send(1)
@@ -549,8 +599,8 @@
                 dma((N // GROUP,)),
                 dma((9,)),
                 dma((RING,)),
-                dma((NA + NA // 2,)),
-                dma((NA + NA // 2,)),
+                dma((NA + NA // 2 + 1,)),
+                dma((NA + NA // 2 + 1,)),
                 dma((NB + NB // 2,)),
                 dma((2 * NC + 2,)),
                 dma((4,)),

time: 47.5 us -> 47 us (0.989)
  Pallas kernels: 46.8 us -> 46.2 us
    pallas_call x1, Pallas kernels: 46.8 us -> 46.2 us  [body(): pl.pallas_call(kernel, out_shape=pltpu.VMEM((tok, half), BF16), in_specs=...]
where the time goes in v7:
time: 47 us; the launch traced here: 46.9 us
  Pallas kernels  46.2 us (98%)
  local copies, waits for them, and re-layouts  0.65 us (1%)
    pallas_call x1, Pallas kernels, body(): pl.pallas_call(kernel, out_shape=pltpu.VMEM((tok, half), BF16), in_specs=...  46.2 us

profile of v7, /device:TPU:0, one launch (start us, length us, event | category | flops | bytes accessed | tf_op | source)
XLA Modules:
  0.0 46.9 jit_solution(12218681209991685571)
XLA Ops:
  0.0 46.2 %shard_map.46 = bf16[24,2560]{1,0:T(8,128)(2,1)S(1)} custom-call(bf16[24,2560]{1,0:T(8,128)(2,1)} %x_hbm.1, f32[2560]{0:T(1024)} %gain_hbm.1, bf16[1280,10240]{1,0:T(8,128)(2,1)} %w_in_hbm.1, bf16[5120,2560]{1,0:T(8,128)(2,1)} %w_out_hbm.1), custom_call_target="tpu_custom_call" | custom-call | tf_op jit(solution)/shard_map/pallas_call | solution.py:569
  46.2 0.7 %copy.6 = bf16[24,2560]{1,0:T(8,128)(2,1)} copy(bf16[24,2560]{1,0:T(8,128)(2,1)S(1)} %shard_map.46) | data formatting | bytes 245760

commit v8 on v7

--- a/solution.py
+++ b/solution.py
@@ -469,11 +469,15 @@
         c_step(4, FIRST)
         b_step(0, FIRST)
         a_step(NF + 2, 2)
-        loop(1, NB, lambda i: b_step(i, FIRST))
+        loop(1, NB - 1, lambda i: b_step(i, FIRST))
+        make_h(NF + 4, 2, a0)
+        b_step(NB - 1, FIRST)
         end_start(0)
-        a_step(NF + 4, 2)
+        make_h(NA - 2, 1, a0)
+        down(NF + 4, a0 + NF + 4, 2)
+        make_h(NA - 1, 1, a0)
         end_send(0)
-        loop(NA - 2, NA, lambda j: a_step(j, 1))
+        loop(NA - 2, NA, lambda j: down(j, a0 + j, 1))
         c_step(0, 3)
         c_step(3, 2)
         loop(0, 2, lambda m: b_step(2 * m, 2))
@@ -516,8 +520,8 @@
         end_start(0)
         c_step(0, 3)
         c_step(3, 2)
+        end_send(0)
         b_step(0, 2)
-        end_send(0)
         a_step(NF, 2)
         b_step(2, 2)
         loop(1, 3, lambda m: a_step(NF + 2 * m, 2))

time: 47 us -> 46.6 us (level)
  no operation moved by 1% of the time
where the time goes in v8:
time: 46.6 us; the launch traced here: 46.5 us
  Pallas kernels  45.8 us (98%)
  local copies, waits for them, and re-layouts  0.65 us (1%)
    pallas_call x1, Pallas kernels, body(): pl.pallas_call(kernel, out_shape=pltpu.VMEM((tok, half), BF16), in_specs=...  45.8 us

profile of v8, /device:TPU:0, one launch (start us, length us, event | category | flops | bytes accessed | tf_op | source)
XLA Modules:
  0.0 46.5 jit_solution(10182386102974818008)
XLA Ops:
  0.0 45.8 %shard_map.46 = bf16[24,2560]{1,0:T(8,128)(2,1)S(1)} custom-call(bf16[24,2560]{1,0:T(8,128)(2,1)} %x_hbm.1, f32[2560]{0:T(1024)} %gain_hbm.1, bf16[1280,10240]{1,0:T(8,128)(2,1)} %w_in_hbm.1, bf16[5120,2560]{1,0:T(8,128)(2,1)} %w_out_hbm.1), custom_call_target="tpu_custom_call" | custom-call | tf_op jit(solution)/shard_map/pallas_call | solution.py:573
  45.8 0.7 %copy.6 = bf16[24,2560]{1,0:T(8,128)(2,1)} copy(bf16[24,2560]{1,0:T(8,128)(2,1)S(1)} %shard_map.46) | data formatting | bytes 245760

commit v9 on v7

--- a/solution.py
+++ b/solution.py
@@ -16,7 +16,8 @@
 NC = 5
 NA = 11
 N = NA + NB + NC
-NF = 3
+NF = 4
+EARLY = 2 * NB
 GROUP = 5
 RING = 8
 TA = 16
@@ -98,6 +99,7 @@
         return jnp.where(lane == 0, jnp.sum(v, axis=1, keepdims=True), jnp.sum(v * v, axis=1, keepdims=True))
 
     me = 4 * y + row
+    stat_g[me, :, :tok] = jnp.transpose(jnp.concatenate([row_sums(xa_v), row_sums(xb_v)], axis=0))[:8]
     with jax.named_scope('barrier'):
         pl.semaphore_wait(barrier, 7)
 
@@ -113,48 +115,37 @@
         return remote(stat_g.at[me], stat_g.at[me], stat_ssem, stat_rsem, (dp, ty, tr))
 
     gain_cp = remote(gain_v.at[0], gain_v.at[1], misc_sem.at[2], misc_sem.at[3], y_next)
-    def to_relay(tk):
-        return remote(xb_v.at[:, pl.ds(feat * tk, feat)], x_relay.at[tk], z_ssem, misc_sem.at[9], y_next)
-
-    def from_relay(tk):
-        return remote(x_relay.at[tk], x_gb.at[row], z_ssem, zb_rsem, (dp, y, 2 * (1 - x) + tk))
+    half_cols = pl.ds(pl.multiple_of(feat * (1 - k), 128), feat)
+    to_relay = remote(xa_v.at[:, half_cols], x_relay, z_ssem, misc_sem.at[9], y_next)
+    from_relay = remote(x_relay, x_ga.at[row], z_ssem, za_rsem, (dp, y, 2 * (1 - x) + 1 - k))
+
+    for d in range(1, 8):
+        stat_copy(d).start()
 
     @pl.when(home == 0)
     def _():
-        to_relay(0).start()
-        to_relay(1).start()
+        to_relay.start()
+        tok_copy(1, 1, 0).start()
+        tok_copy(1, 1, 1).start()
+        tok_copy(1, 0, 0).start()
+        tok_copy(1, 0, 1).start()
         tok_copy(0, 1, 0).start()
+        tok_copy(0, 0, 0).start()
+        tok_copy(0, 0, 1).start()
 
     @pl.when(home == 1)
     def _():
         gain_cp.start()
-        tok_copy(0, 0, 1).start()
-        tok_copy(0, 1, 0).start()
-
-    stat_g[me, :, :tok] = jnp.transpose(jnp.concatenate([row_sums(xa_v), row_sums(xb_v)], axis=0))[:8]
-    for d in range(1, 8):
-        stat_copy(d).start()
-
-    @pl.when(home == 0)
-    def _():
-        tok_copy(0, 1, 1).start()
-        for group in range(2):
-            tok_copy(group, 0, 0).start()
+        for group in (1, 0):
             tok_copy(group, 0, 1).start()
-
-    @pl.when(home == 1)
-    def _():
-        tok_copy(0, 1, 1).start()
-        tok_copy(1, 0, 1).start()
-        tok_copy(1, 1, 0).start()
-        tok_copy(1, 1, 1).start()
+            tok_copy(group, 1, 0).start()
+            tok_copy(group, 1, 1).start()
         x_ga[row] = jnp.where(k == 0, xa_v[:, :feat], xa_v[:, feat:])
         x_gb[row] = jnp.where(k == 0, xb_v[:, :feat], xb_v[:, feat:])
         gain_v[1] = gain_v[0]
         with jax.named_scope('x_relay_wait'):
-            remote(x_relay, x_relay, z_ssem, misc_sem.at[9], y_next).wait_recv()
-        from_relay(0).start()
-        from_relay(1).start()
+            to_relay.wait_recv()
+        from_relay.start()
 
     @pl.when(home == 0)
     def _():
@@ -201,8 +192,14 @@
     def d_copy(p, part, seq):
         return remote(part_of(d_send, p, part), part_of(d_recv, p, part), d_ssem, d_rsem.at[seq % RING], sibling)
 
+    def b_index(j, part):
+        return NA + j // 2 if part == 2 else j + 7
+
+    def x_group(j, part, first, sem):
+        return remote(part_of(own, first + j, part), part_of(x_recv, j, part), x_ssem, x_rsem.at[sem], x_next)
+
     def x_copy_of(j, part, first):
-        sem = x_rsem.at[NA + j // 2] if part > 0 else x_rsem.at[j]
+        sem = x_rsem.at[b_index(j, part)] if part > 0 else x_rsem.at[j]
         return remote(part_of(own, first + j, part), part_of(x_recv, j, part), x_ssem, sem, x_next)
 
     def c_copy(j):
@@ -238,102 +235,94 @@
             group = w_in_v.at[pl.ds(p, GROUP)]
             pltpu.make_async_copy(group, group, w_in_sem.at[p // GROUP]).wait()
 
+    def pair_group(p, part, seq):
+        pair_add(p, part, seq)
+        q = chunk_of(p)
+
+        @pl.when((q >= c0) & (q < a0))
+        def _():
+            c_part(q - c0, part).start()
+
+        @pl.when((home == 1) & (q < c0))
+        def _():
+            x_group(q, part, 0, NA + q // 2 if part else q).start()
+
+        @pl.when((home == 0) & (q >= a0))
+        def _():
+            x_group(q - a0, part, a0, q - a0).start()
+
     def pair_sum(p):
-        pair_add(p, WHOLE, p + 2)
+        pair_add(p, WHOLE, p + EARLY)
         q = chunk_of(p)
 
         @pl.when((q >= c0) & (q < a0))
         def _():
             c_copy(q - c0).start()
 
-        @pl.when((home == 1) & (q < c0))
-        def _():
-            x_copy_of(q, FIRST, 0).start()
-
-            @pl.when(q % 2 == 1)
+        @pl.when((home == 0) & (q >= a0))
+        def _():
+            x_copy_of(q - a0, FIRST, a0).start()
+
+    def up_early(part, seq):
+        def step(p, _):
+            if part:
+                @pl.when(p % GROUP == 0)
+                def _():
+                    wait_w_in(p)
+            up(p, part, p + seq)
+
+            @pl.when(p >= 2)
             def _():
-                x_copy_of(q - 1, 2, 0).start()
-
-        @pl.when((home == 0) & (q >= a0 + NF))
-        def _():
-            x_copy_of(q - a0, FIRST, a0).start()
-
-        @pl.when((home == 0) & (q >= a0) & (q < a0 + NF))
-        def _():
-            x_copy_of(q - a0, WHOLE, a0).start()
+                pair_group(p - 2, part, p - 2 + seq)
+
+            if part == FIRST:
+                w_out_copy(p).start()
+            return 0
+
+        lax.fori_loop(0, EARLY, step, 0)
 
     def up_step(p, _):
         @pl.when(p % GROUP == 0)
         def _():
             wait_w_in(p)
-        up(p, WHOLE, p + 2)
+        up(p, WHOLE, p + EARLY)
         w_out_copy(p).start()
 
-        @pl.when(p >= 4)
+        @pl.when(p >= EARLY + 2)
         def _():
             pair_sum(p - 2)
 
-        @pl.when((p >= 2) & (p < 4))
-        def _():
-            pair_add(p - 2, 1, p)
-
-            @pl.when(p == 3)
-            def _():
-                c_part(0, 1).start()
-
-            @pl.when((p == 2) & (home == 0))
-            def _():
-                first_b_part().start()
-
-        @pl.when((p == 13) & (home == 1))
+        @pl.when(p < EARLY + 2)
+        def _():
+            pair_group(p - 2, FIRST, p - 2 + EARLY)
+
+        @pl.when((p == 17) & (home == 1))
         def _():
             pass_c(0)
-
-        @pl.when((p == 18) & (home == 1))
-        def _():
-            pass_c(1)
         return 0
 
-    def first_b_part():
-        return remote(part_of(own, a0, 1), part_of(x_recv, 0, 1), x_ssem, x_rsem.at[0], x_next)
-
+    make_z(1)
+    up_early(1, 0)
+    pair_group(EARLY - 2, 1, EARLY - 2)
+    pair_group(EARLY - 1, 1, EARLY - 1)
     make_z(0)
-    wait_w_in(0)
-    up(0, FIRST, 0)
-    up(1, FIRST, 1)
-    make_z(1)
-    up(0, 1, 2)
-    w_out_copy(0).start()
-    pair_add(0, FIRST, 0)
-
-    @pl.when(home == 1)
-    def _():
-        x_copy_of(0, FIRST, 0).start()
+    up_early(FIRST, EARLY)
+    lax.fori_loop(EARLY, N, up_step, 0)
+    pair_sum(N - 2)
+    pair_sum(N - 1)
 
     @pl.when(home == 0)
     def _():
-        x_copy_of(0, FIRST, a0).start()
-
-    up(1, 1, 3)
-    w_out_copy(1).start()
-    pair_add(1, FIRST, 1)
-    c_part(0, FIRST).start()
-    lax.fori_loop(2, N, up_step, 0)
-    pair_sum(N - 2)
-    pair_sum(N - 1)
-
-    @pl.when(home == 0)
-    def _():
-        for j in range(NF, NA - 2, 2):
-            x_copy_of(j, 2, a0).start()
-        x_copy_of(NA - 2, 1, a0).start()
-        x_copy_of(NA - 1, 1, a0).start()
+        x_copy_of(NF, 2, a0).start()
+        x_copy_of(NF + 2, 2, a0).start()
+        for j in range(NF + 4, NA):
+            x_copy_of(j, 1, a0).start()
 
     with jax.named_scope('w_out_wait'):
         pltpu.make_async_copy(w_out_v, w_out_v, w_out_sem).wait()
 
     def y_copy(j, part):
-        sem = y_rsem.at[NA + j // 2] if part > 0 else y_rsem.at[j]
+        sem = y_rsem.at[b_index(j, part)] if part > 0 else y_rsem.at[j]
         return remote(part_of(hall, j, part), part_of(hall, NA + j, part), y_ssem, sem, y_next)
 
     def b_sem(j, part):
@@ -434,46 +423,62 @@
             make_h(j, part, a0)
             down(j, a0 + j, part)
 
-        loop(0, NF, lambda j: a_step(j, WHOLE))
+        pass_c(1)
 
         def step(j):
-            for t, i in ((3, 2), (4, 3), (6, 4)):
+            @pl.when(j == 2)
+            def _():
+                pass_c(2)
+            a_step(j, WHOLE)
+
+        loop(0, NF, step)
+
+        def step(j):
+            for t, i in ((4, 3), (6, 4)):
                 @pl.when(j == t)
                 def _():
                     pass_c(i)
 
-            @pl.when(j == 8)
+            @pl.when(j == 7)
             def _():
                 relay(0, FIRST)
                 relay(1, FIRST)
             a_step(j, FIRST)
 
-        loop(NF, 9, step)
+        loop(NF, 8, step)
         relay(2, FIRST)
         relay(3, FIRST)
         c_relay(0, 3).start()
         c_relay(3, 2).start()
 
         def step(t):
-            a_step(9 + t, FIRST)
+            a_step(8 + t, FIRST)
 
             @pl.when(t == 0)
             def _():
                 relay(0, 2)
                 relay(2, 2)
+
+            @pl.when(t == 1)
+            def _():
+                c_step(1, FIRST)
             c_step(2 * t, FIRST)
-            c_step(2 * t + 1, FIRST)
 
         loop(0, 2, step)
+        a_step(10, FIRST)
+        loop(3, 5, lambda i: c_step(i, FIRST))
         a_step(NF, 2)
-        c_step(4, FIRST)
-        b_step(0, FIRST)
+        loop(0, 2, lambda i: b_step(i, FIRST))
         a_step(NF + 2, 2)
-        loop(1, NB, lambda i: b_step(i, FIRST))
+        b_step(2, FIRST)
+        make_h(NF + 4, 1, a0)
+        b_step(NB - 1, FIRST)
         end_start(0)
-        a_step(NF + 4, 2)
+        make_h(NF + 5, 1, a0)
+        down(NF + 4, a0 + NF + 4, 1)
+        make_h(NF + 6, 1, a0)
         end_send(0)
-        loop(NA - 2, NA, lambda j: a_step(j, 1))
+        loop(NF + 5, NA, lambda j: down(j, a0 + j, 1))
         c_step(0, 3)
         c_step(3, 2)
         loop(0, 2, lambda m: b_step(2 * m, 2))
@@ -504,24 +509,22 @@
             a_step(t, WHOLE)
 
         loop(0, NF, step)
-        a_step(NF, FIRST)
-        c_step(4, FIRST)
 
         def step(t):
-            a_step(NF + 1 + t, FIRST)
             b_step(t, FIRST)
+            a_step(NF + t, FIRST)
 
         loop(0, 4, step)
-        loop(NF + 5, NA, lambda j: a_step(j, FIRST))
+        a_step(8, FIRST)
+        c_step(0, 3)
+        loop(9, NA, lambda j: a_step(j, FIRST))
         end_start(0)
-        c_step(0, 3)
         c_step(3, 2)
         b_step(0, 2)
         end_send(0)
-        a_step(NF, 2)
         b_step(2, 2)
-        loop(1, 3, lambda m: a_step(NF + 2 * m, 2))
-        loop(NA - 2, NA, lambda j: a_step(j, 1))
+        loop(0, 2, lambda m: a_step(NF + 2 * m, 2))
+        loop(NF + 4, NA, lambda j: a_step(j, 1))
 
     end_start(1)
     end_send(1)
@@ -547,9 +550,8 @@
         @pl.when(home == 1)
         def _():
             gain_cp.wait_send()
-            sent(x_ga.at[pl.ds(0, 3)], z_ssem)
-            sent(x_gb, z_ssem)
-            sent(x_gb.at[0], z_ssem)
+            sent(x_ga, z_ssem)
+            sent(x_gb.at[pl.ds(0, 3)], z_ssem)
             sent(own.at[pl.ds(0, NB)], x_ssem)
             sent(c_recv.at[1], c_ssem)
             sent(hall.at[pl.ds(0, NA)], y_ssem)
@@ -578,7 +580,7 @@
                 pltpu.VMEM((8, 8, 128), F32),
                 pltpu.VMEM((4, TA, feat), BF16),
                 pltpu.VMEM((4, tok - TA, feat), BF16),
-                pltpu.VMEM((2, tok - TA, feat), BF16),
+                pltpu.VMEM((TA, feat), BF16),
                 pltpu.VMEM((tokens, feat), BF16),
                 pltpu.VMEM((N, feat, 2 * C), BF16),
                 pltpu.VMEM((N, C, half), BF16),
@@ -599,8 +601,8 @@
                 dma((N // GROUP,)),
                 dma((9,)),
                 dma((RING,)),
-                dma((NA + NA // 2 + 1,)),
-                dma((NA + NA // 2 + 1,)),
+                dma((NA + 7,)),
+                dma((NA + 7,)),
                 dma((NB + NB // 2,)),
                 dma((2 * NC + 2,)),
                 dma((4,)),

time: 47 us -> 48.3 us (1.028)
  Pallas kernels: 46.2 us -> 47.5 us
    pallas_call x1, Pallas kernels: 46.2 us -> 47.5 us  [body(): pl.pallas_call(kernel, out_shape=pltpu.VMEM((tok, half), BF16), in_specs=...]
where the time goes in v9:
time: 48.3 us; the launch traced here: 48.2 us
  Pallas kernels  47.5 us (98%)
  local copies, waits for them, and re-layouts  0.65 us (1%)
    pallas_call x1, Pallas kernels, body(): pl.pallas_call(kernel, out_shape=pltpu.VMEM((tok, half), BF16), in_specs=...  47.5 us

profile of v9, /device:TPU:0, one launch (start us, length us, event | category | flops | bytes accessed | tf_op | source)
XLA Modules:
  0.0 48.2 jit_solution(12478985964948437816)
XLA Ops:
  0.0 47.5 %shard_map.46 = bf16[24,2560]{1,0:T(8,128)(2,1)S(1)} custom-call(bf16[24,2560]{1,0:T(8,128)(2,1)} %x_hbm.1, f32[2560]{0:T(1024)} %gain_hbm.1, bf16[1280,10240]{1,0:T(8,128)(2,1)} %w_in_hbm.1, bf16[5120,2560]{1,0:T(8,128)(2,1)} %w_out_hbm.1), custom_call_target="tpu_custom_call" | custom-call | tf_op jit(solution)/shard_map/pallas_call | solution.py:571
  47.5 0.7 %copy.6 = bf16[24,2560]{1,0:T(8,128)(2,1)} copy(bf16[24,2560]{1,0:T(8,128)(2,1)S(1)} %shard_map.46) | data formatting | bytes 245760

commit v10 on v9

--- a/solution.py
+++ b/solution.py
@@ -17,9 +17,10 @@
 NA = 11
 N = NA + NB + NC
 NF = 4
-EARLY = 2 * NB
+EARLY = 4
 GROUP = 5
-RING = 8
+LAG = 3
+RING = 12
 TA = 16
 
 
@@ -259,57 +260,53 @@
         def _():
             c_copy(q - c0).start()
 
-        @pl.when((home == 0) & (q >= a0))
+        @pl.when((home == 1) & (q < c0))
+        def _():
+            x_copy_of(q, FIRST, 0).start()
+
+            @pl.when(q % 2 == 1)
+            def _():
+                x_copy_of(q - 1, 2, 0).start()
+
+        @pl.when((home == 0) & (q >= a0 + NF))
         def _():
             x_copy_of(q - a0, FIRST, a0).start()
 
-    def up_early(part, seq):
+        @pl.when((home == 0) & (q >= a0) & (q < a0 + NF))
+        def _():
+            x_copy_of(q - a0, WHOLE, a0).start()
+
+    def up_loop(lo, hi, part, seq, then):
         def step(p, _):
-            if part:
+            if part != FIRST:
                 @pl.when(p % GROUP == 0)
                 def _():
                     wait_w_in(p)
             up(p, part, p + seq)
-
-            @pl.when(p >= 2)
-            def _():
-                pair_group(p - 2, part, p - 2 + seq)
-
-            if part == FIRST:
+            if part != 1:
                 w_out_copy(p).start()
+            then(p)
             return 0
 
-        lax.fori_loop(0, EARLY, step, 0)
-
-    def up_step(p, _):
-        @pl.when(p % GROUP == 0)
-        def _():
-            wait_w_in(p)
-        up(p, WHOLE, p + EARLY)
-        w_out_copy(p).start()
-
-        @pl.when(p >= EARLY + 2)
-        def _():
-            pair_sum(p - 2)
-
-        @pl.when(p < EARLY + 2)
-        def _():
-            pair_group(p - 2, FIRST, p - 2 + EARLY)
+        lax.fori_loop(lo, hi, step, 0)
+
+    def late(p):
+        pair_sum(p - LAG)
 
         @pl.when((p == 17) & (home == 1))
         def _():
             pass_c(0)
-        return 0
 
     make_z(1)
-    up_early(1, 0)
-    pair_group(EARLY - 2, 1, EARLY - 2)
-    pair_group(EARLY - 1, 1, EARLY - 1)
+    up_loop(0, EARLY, 1, 0, lambda p: None)
+    pair_group(0, 1, 0)
     make_z(0)
-    up_early(FIRST, EARLY)
-    lax.fori_loop(EARLY, N, up_step, 0)
-    pair_sum(N - 2)
-    pair_sum(N - 1)
+    up_loop(0, LAG, FIRST, EARLY, lambda p: pair_group(p + 1, 1, p + 1))
+    up_loop(LAG, EARLY, FIRST, EARLY, lambda p: pair_group(p - LAG, FIRST, p - LAG + EARLY))
+    up_loop(EARLY, EARLY + LAG, WHOLE, EARLY, lambda p: pair_group(p - LAG, FIRST, p - LAG + EARLY))
+    up_loop(EARLY + LAG, N, WHOLE, EARLY, late)
+    for p in range(N - LAG, N):
+        pair_sum(p)
 
     @pl.when(home == 0)
     def _():
@@ -386,6 +383,11 @@
             e_copy(group, 0).wait_recv()
         f_send[group][...] = acc[token_rows(group, 2 * (1 - x) + k), :] + e_recv[group][0]
         f_copy(group).start()
+
+    def end_send_from(core):
+        @pl.when(k == core)
+        def _():
+            end_send(0)
 
     def end_sum(group):
         with jax.named_scope('e1_wait'):
@@ -477,8 +479,9 @@
         make_h(NF + 5, 1, a0)
         down(NF + 4, a0 + NF + 4, 1)
         make_h(NF + 6, 1, a0)
-        end_send(0)
+        end_send_from(0)
         loop(NF + 5, NA, lambda j: down(j, a0 + j, 1))
+        end_send_from(1)
         c_step(0, 3)
         c_step(3, 2)
         loop(0, 2, lambda m: b_step(2 * m, 2))
@@ -520,10 +523,11 @@
         loop(9, NA, lambda j: a_step(j, FIRST))
         end_start(0)
         c_step(3, 2)
-        b_step(0, 2)
-        end_send(0)
-        b_step(2, 2)
-        loop(0, 2, lambda m: a_step(NF + 2 * m, 2))
+        end_send_from(0)
+        loop(0, 2, lambda m: b_step(2 * m, 2))
+        a_step(NF, 2)
+        end_send_from(1)
+        a_step(NF + 2, 2)
         loop(NF + 4, NA, lambda j: a_step(j, 1))
 
     end_start(1)

time: 48.3 us -> 45.2 us (0.936)
  Pallas kernels: 47.5 us -> 44.5 us
    pallas_call x1, Pallas kernels: 47.5 us -> 44.5 us  [body(): pl.pallas_call(kernel, out_shape=pltpu.VMEM((tok, half), BF16), in_specs=...]
where the time goes in v10:
time: 45.2 us; the launch traced here: 45.1 us
  Pallas kernels  44.5 us (98%)
  local copies, waits for them, and re-layouts  0.65 us (1%)
    pallas_call x1, Pallas kernels, body(): pl.pallas_call(kernel, out_shape=pltpu.VMEM((tok, half), BF16), in_specs=...  44.5 us

profile of v10, /device:TPU:0, one launch (start us, length us, event | category | flops | bytes accessed | tf_op | source)
XLA Modules:
  0.0 45.1 jit_solution(9557393664876039961)
XLA Ops:
  0.0 44.5 %shard_map.46 = bf16[24,2560]{1,0:T(8,128)(2,1)S(1)} custom-call(bf16[24,2560]{1,0:T(8,128)(2,1)} %x_hbm.1, f32[2560]{0:T(1024)} %gain_hbm.1, bf16[1280,10240]{1,0:T(8,128)(2,1)} %w_in_hbm.1, bf16[5120,2560]{1,0:T(8,128)(2,1)} %w_out_hbm.1), custom_call_target="tpu_custom_call" | custom-call | tf_op jit(solution)/shard_map/pallas_call | solution.py:575
  44.5 0.7 %copy.6 = bf16[24,2560]{1,0:T(8,128)(2,1)} copy(bf16[24,2560]{1,0:T(8,128)(2,1)S(1)} %shard_map.46) | data formatting | bytes 245760

commit v11 on v10

--- a/solution.py
+++ b/solution.py
@@ -18,9 +18,9 @@
 N = NA + NB + NC
 NF = 4
 EARLY = 4
-GROUP = 5
+GROUP = 10
 LAG = 3
-RING = 12
+RING = 8
 TA = 16
 
 
@@ -29,7 +29,8 @@
            acc, ea_recv, eb_recv, fa_send, fa_recv, fb_send, fb_recv,
            misc_sem, w_in_sem, send_sem, d_rsem, x_rsem, y_rsem, b_rsem, c_rsem, e_rsem, f_rsem):
     w_out_sem, stat_rsem, za_rsem, zb_rsem = [misc_sem.at[i] for i in range(4, 8)]
-    stat_ssem, z_ssem, d_ssem, x_ssem, y_ssem, b_ssem, c_ssem, e_ssem, f_ssem = [send_sem.at[i] for i in range(9)]
+    stat_ssem = z_ssem = d_ssem = x_ssem = y_ssem = b_ssem = c_ssem = e_ssem = send_sem.at[0]
+    f_ssem = send_sem.at[1]
     y = lax.axis_index("col")
     row = lax.axis_index("row")
     x = row // 2
@@ -115,9 +116,9 @@
         tr = (row + d % 4) % 4
         return remote(stat_g.at[me], stat_g.at[me], stat_ssem, stat_rsem, (dp, ty, tr))
 
-    gain_cp = remote(gain_v.at[0], gain_v.at[1], misc_sem.at[2], misc_sem.at[3], y_next)
+    gain_cp = remote(gain_v.at[0], gain_v.at[1], z_ssem, misc_sem.at[3], y_next)
     half_cols = pl.ds(pl.multiple_of(feat * (1 - k), 128), feat)
-    to_relay = remote(xa_v.at[:, half_cols], x_relay, z_ssem, misc_sem.at[9], y_next)
+    to_relay = remote(xa_v.at[:, half_cols], x_relay, z_ssem, misc_sem.at[2], y_next)
     from_relay = remote(x_relay, x_ga.at[row], z_ssem, za_rsem, (dp, y, 2 * (1 - x) + 1 - k))
 
     for d in range(1, 8):
@@ -194,7 +195,7 @@
         return remote(part_of(d_send, p, part), part_of(d_recv, p, part), d_ssem, d_rsem.at[seq % RING], sibling)
 
     def b_index(j, part):
-        return NA + j // 2 if part == 2 else j + 7
+        return 9 + j // 2 if part == 2 else j + 5
 
     def x_group(j, part, first, sem):
         return remote(part_of(own, first + j, part), part_of(x_recv, j, part), x_ssem, x_rsem.at[sem], x_next)
@@ -246,7 +247,7 @@
 
         @pl.when((home == 1) & (q < c0))
         def _():
-            x_group(q, part, 0, NA + q // 2 if part else q).start()
+            x_group(q, part, 0, 9 + q // 2 if part else q).start()
 
         @pl.when((home == 0) & (q >= a0))
         def _():
@@ -352,7 +353,7 @@
         yc_copy(j, part).start()
 
     def yc_copy(j, part):
-        sem = y_rsem.at[NA + 2 + j // 3] if part > 0 else y_rsem.at[c0 + j]
+        sem = y_rsem.at[NA + j // 3] if part > 0 else y_rsem.at[c0 + j]
         return remote(part_of(hall, c0 + j, part), part_of(hall, NA + c0 + j, part), y_ssem, sem, y_next)
 
     def down(slot, i, part):
@@ -493,10 +494,13 @@
                 y_copy(j, part).wait_recv()
             down(NA + j, a0 + j, part)
 
-        def b_step(i, part):
+        def b_pass(i, part):
             with jax.named_scope('b_wait'):
                 relay_copy(i, part).wait_recv()
             back_copy(i, part).start()
+
+        def b_step(i, part):
+            b_pass(i, part)
             down(2 * NA + i, i, part)
 
         def c_step(i, part):
@@ -518,13 +522,15 @@
             a_step(NF + t, FIRST)
 
         loop(0, 4, step)
-        a_step(8, FIRST)
+        loop(8, 10, lambda j: a_step(j, FIRST))
         c_step(0, 3)
-        loop(9, NA, lambda j: a_step(j, FIRST))
+        a_step(10, FIRST)
         end_start(0)
+        end_send_from(0)
         c_step(3, 2)
-        end_send_from(0)
-        loop(0, 2, lambda m: b_step(2 * m, 2))
+        b_pass(0, 2)
+        b_pass(2, 2)
+        down(2 * NA, 0, 4)
         a_step(NF, 2)
         end_send_from(1)
         a_step(NF + 2, 2)
@@ -601,12 +607,12 @@
                 pltpu.VMEM((TA, half), F32),
                 pltpu.VMEM((tok - TA, half), F32),
                 pltpu.VMEM((tok - TA, half), F32),
-                dma((10,)),
+                dma((9,)),
                 dma((N // GROUP,)),
-                dma((9,)),
+                dma((2,)),
                 dma((RING,)),
-                dma((NA + 7,)),
-                dma((NA + 7,)),
+                dma((NA + 5,)),
+                dma((NA + 5,)),
                 dma((NB + NB // 2,)),
                 dma((2 * NC + 2,)),
                 dma((4,)),

time: 45.2 us -> 45 us (level)
  no operation moved by 1% of the time
where the time goes in v11:
time: 45 us; the launch traced here: 44.9 us
  Pallas kernels  44.2 us (98%)
  local copies, waits for them, and re-layouts  0.65 us (1%)
    pallas_call x1, Pallas kernels, body(): pl.pallas_call(kernel, out_shape=pltpu.VMEM((tok, half), BF16), in_specs=...  44.2 us

profile of v11, /device:TPU:0, one launch (start us, length us, event | category | flops | bytes accessed | tf_op | source)
XLA Modules:
  0.0 44.9 jit_solution(6902847691483971152)
XLA Ops:
  0.0 44.2 %shard_map.46 = bf16[24,2560]{1,0:T(8,128)(2,1)S(1)} custom-call(bf16[24,2560]{1,0:T(8,128)(2,1)} %x_hbm.1, f32[2560]{0:T(1024)} %gain_hbm.1, bf16[1280,10240]{1,0:T(8,128)(2,1)} %w_in_hbm.1, bf16[5120,2560]{1,0:T(8,128)(2,1)} %w_out_hbm.1), custom_call_target="tpu_custom_call" | custom-call | tf_op jit(solution)/shard_map/pallas_call | solution.py:581
  44.3 0.7 %copy.6 = bf16[24,2560]{1,0:T(8,128)(2,1)} copy(bf16[24,2560]{1,0:T(8,128)(2,1)S(1)} %shard_map.46) | data formatting | bytes 245760

commit v12 on v11

--- a/solution.py
+++ b/solution.py
@@ -17,10 +17,10 @@
 NA = 11
 N = NA + NB + NC
 NF = 4
-EARLY = 4
+EARLY = 6
 GROUP = 10
 LAG = 3
-RING = 8
+RING = 10
 TA = 16
 
 
@@ -101,7 +101,7 @@
         return jnp.where(lane == 0, jnp.sum(v, axis=1, keepdims=True), jnp.sum(v * v, axis=1, keepdims=True))
 
     me = 4 * y + row
-    stat_g[me, :, :tok] = jnp.transpose(jnp.concatenate([row_sums(xa_v), row_sums(xb_v)], axis=0))[:8]
+    stat_g[me, :, :tok] = jnp.transpose(jnp.concatenate([row_sums(xa_v), row_sums(xb_v)], axis=0))[:2]
     with jax.named_scope('barrier'):
         pl.semaphore_wait(barrier, 7)
 
@@ -173,7 +173,8 @@
 
         t0, n, base = ((0, TA, 0), (TA, tb, rows_a))[group]
         for src in range(4):
-            st = jnp.transpose(stat_g[src] + stat_g[4 + src])[t0:t0 + n] * (1.0 / (2 * half))
+            both = stat_g[src] + stat_g[4 + src]
+            st = jnp.transpose(jnp.concatenate([both] * 4, axis=0))[t0:t0 + n] * (1.0 / (2 * half))
             mean = st[:, 0:1]
             var = st[:, 1:2] - mean * mean
             z = (ref[src].astype(F32) - mean) * lax.rsqrt(var + NORM_EPS) * gain
@@ -265,9 +266,7 @@
         def _():
             x_copy_of(q, FIRST, 0).start()
 
-            @pl.when(q % 2 == 1)
-            def _():
-                x_copy_of(q - 1, 2, 0).start()
+            x_group(q, 1, 0, 9 + q // 2).start()
 
         @pl.when((home == 0) & (q >= a0 + NF))
         def _():
@@ -298,11 +297,16 @@
         def _():
             pass_c(0)
 
+    def flush(p):
+        for i in range(2):
+            pair_group(2 * p + 2 + i, 1, 2 * p + 2 + i)
+
     make_z(1)
-    up_loop(0, EARLY, 1, 0, lambda p: None)
-    pair_group(0, 1, 0)
+    up_loop(0, 4, 1, 0, lambda p: None)
+    up_loop(4, EARLY, 1, 0, lambda p: pair_group(p - 4, 1, p - 4))
     make_z(0)
-    up_loop(0, LAG, FIRST, EARLY, lambda p: pair_group(p + 1, 1, p + 1))
+    up_loop(0, 2, FIRST, EARLY, flush)
+    up_loop(2, LAG, FIRST, EARLY, lambda p: None)
     up_loop(LAG, EARLY, FIRST, EARLY, lambda p: pair_group(p - LAG, FIRST, p - LAG + EARLY))
     up_loop(EARLY, EARLY + LAG, WHOLE, EARLY, lambda p: pair_group(p - LAG, FIRST, p - LAG + EARLY))
     up_loop(EARLY + LAG, N, WHOLE, EARLY, late)
@@ -587,7 +591,7 @@
                 pltpu.VMEM((TA, half), BF16),
                 pltpu.VMEM((tok - TA, half), BF16),
                 pltpu.VMEM((2, half), F32),
-                pltpu.VMEM((8, 8, 128), F32),
+                pltpu.VMEM((8, 2, 128), F32),
                 pltpu.VMEM((4, TA, feat), BF16),
                 pltpu.VMEM((4, tok - TA, feat), BF16),
                 pltpu.VMEM((TA, feat), BF16),

time: 45 us -> 44.8 us (level)
  no operation moved by 1% of the time
where the time goes in v12:
time: 44.8 us; the launch traced here: 44.7 us
  Pallas kernels  44 us (98%)
  local copies, waits for them, and re-layouts  0.65 us (1%)
    pallas_call x1, Pallas kernels, body(): pl.pallas_call(kernel, out_shape=pltpu.VMEM((tok, half), BF16), in_specs=...  44 us

profile of v12, /device:TPU:0, one launch (start us, length us, event | category | flops | bytes accessed | tf_op | source)
XLA Modules:
  0.0 44.7 jit_solution(7545115462655061018)
XLA Ops:
  0.0 44.0 %shard_map.46 = bf16[24,2560]{1,0:T(8,128)(2,1)S(1)} custom-call(bf16[24,2560]{1,0:T(8,128)(2,1)} %x_hbm.1, f32[2560]{0:T(1024)} %gain_hbm.1, bf16[1280,10240]{1,0:T(8,128)(2,1)} %w_in_hbm.1, bf16[5120,2560]{1,0:T(8,128)(2,1)} %w_out_hbm.1), custom_call_target="tpu_custom_call" | custom-call | tf_op jit(solution)/shard_map/pallas_call | solution.py:585
  44.0 0.7 %copy.6 = bf16[24,2560]{1,0:T(8,128)(2,1)} copy(bf16[24,2560]{1,0:T(8,128)(2,1)S(1)} %shard_map.46) | data formatting | bytes 245760

commit v13 on v12

--- a/solution.py
+++ b/solution.py
@@ -215,6 +215,15 @@
         sem = c_rsem.at[2 * NC + j // 3] if part > 0 else c_rsem.at[NC + j]
         return remote(part_of(c_recv.at[0], j, part), part_of(c_recv.at[1], j, part), c_ssem, sem, x_next)
 
+    last = NA - 1
+
+    def both_home():
+        return remote(part_of(own, a0 + last, 1), part_of(c_recv.at[0], NC, 1), c_ssem, c_rsem.at[2 * NC + 2], y_next)
+
+    def both_far():
+        return remote(part_of(own, a0 + last, 1), part_of(c_recv.at[1], NC, 1), c_ssem, c_rsem.at[2 * NC + 3],
+                      (dp, 1 - y, 2 * (1 - x) + k))
+
     def pass_c(j):
         with jax.named_scope('c_wait'):
             c_copy(j).wait_recv()
@@ -317,8 +326,9 @@
     def _():
         x_copy_of(NF, 2, a0).start()
         x_copy_of(NF + 2, 2, a0).start()
-        for j in range(NF + 4, NA):
-            x_copy_of(j, 1, a0).start()
+        x_copy_of(NF + 4, 2, a0).start()
+        both_far().start()
+        x_copy_of(last, 1, a0).start()
 
     with jax.named_scope('w_out_wait'):
         pltpu.make_async_copy(w_out_v, w_out_v, w_out_sem).wait()
@@ -342,11 +352,12 @@
             total = left(c)[rows, :] + right(c)[rows, :]
             hall[j + c, rows, :] = jax.nn.gelu(total, approximate=True).astype(BF16)
 
-    def make_h(j, part, first):
+    def make_h(j, part, first, send=True):
         with jax.named_scope('x_wait'):
             x_copy_of(j, part, 0).wait_recv()
         put_h(j, part, lambda c: own.at[first + j + c], lambda c: x_recv.at[j + c])
-        y_copy(j, part).start()
+        if send:
+            y_copy(j, part).start()
 
     def make_h_c(j, part):
         with jax.named_scope('c_wait'):
@@ -431,6 +442,7 @@
             down(j, a0 + j, part)
 
         pass_c(1)
+        both_home().start()
 
         def step(j):
             @pl.when(j == 2)
@@ -478,16 +490,15 @@
         loop(0, 2, lambda i: b_step(i, FIRST))
         a_step(NF + 2, 2)
         b_step(2, FIRST)
-        make_h(NF + 4, 1, a0)
         b_step(NB - 1, FIRST)
         end_start(0)
-        make_h(NF + 5, 1, a0)
-        down(NF + 4, a0 + NF + 4, 1)
-        make_h(NF + 6, 1, a0)
+        make_h(NF + 4, 2, a0)
         end_send_from(0)
-        loop(NF + 5, NA, lambda j: down(j, a0 + j, 1))
+        down(NF + 4, a0 + NF + 4, 2)
+        c_step(0, 3)
         end_send_from(1)
-        c_step(0, 3)
+        make_h(last, 1, a0, send=False)
+        down(last, a0 + last, 1)
         c_step(3, 2)
         loop(0, 2, lambda m: b_step(2 * m, 2))
 
@@ -537,8 +548,13 @@
         down(2 * NA, 0, 4)
         a_step(NF, 2)
         end_send_from(1)
+        with jax.named_scope('both_wait'):
+            both_home().wait_recv()
+            both_far().wait_recv()
+        put_h(c0 + NC, 1, lambda c: c_recv.at[0, NC + c], lambda c: c_recv.at[1, NC + c])
+        down(c0 + NC, a0 + last, 1)
         a_step(NF + 2, 2)
-        loop(NF + 4, NA, lambda j: a_step(j, 1))
+        a_step(NF + 4, 2)
 
     end_start(1)
     end_send(1)
@@ -550,7 +566,8 @@
         sent(stat_g.at[pl.ds(0, 7)], stat_ssem)
         sent(d_send, d_ssem)
         sent(hall.at[pl.ds(0, NB)], b_ssem)
-        sent(c_recv.at[0], c_ssem)
+        sent(c_recv.at[0, pl.ds(0, NC)], c_ssem)
+        sent(part_of(own, 0, 1), c_ssem)
         sent(ea_recv, e_ssem)
         sent(eb_recv, e_ssem)
 
@@ -567,8 +584,9 @@
             sent(x_ga, z_ssem)
             sent(x_gb.at[pl.ds(0, 3)], z_ssem)
             sent(own.at[pl.ds(0, NB)], x_ssem)
-            sent(c_recv.at[1], c_ssem)
-            sent(hall.at[pl.ds(0, NA)], y_ssem)
+            sent(c_recv.at[1, pl.ds(0, NC)], c_ssem)
+            sent(hall.at[pl.ds(0, last)], y_ssem)
+            sent(part_of(hall, 0, FIRST), y_ssem)
 
     end_sum(0)
     end_sum(1)
@@ -602,7 +620,7 @@
                 pltpu.VMEM((N, tokens, C), F32),
                 pltpu.VMEM((N, tokens, C), F32),
                 pltpu.VMEM((NA, tokens, C), F32),
-                pltpu.VMEM((2, NC, tokens, C), F32),
+                pltpu.VMEM((2, NC + 1, tokens, C), F32),
                 pltpu.VMEM((2 * NA + NB, tokens, C), BF16),
                 pltpu.VMEM((tokens, half), F32),
                 pltpu.VMEM((2, TA, half), F32),
@@ -618,7 +636,7 @@
                 dma((NA + 5,)),
                 dma((NA + 5,)),
                 dma((NB + NB // 2,)),
-                dma((2 * NC + 2,)),
+                dma((2 * NC + 4,)),
                 dma((4,)),
                 dma((2,)),
             ],

time: 44.8 us -> 44.7 us (level)
  no operation moved by 1% of the time
where the time goes in v13:
time: 44.7 us; the launch traced here: 44.6 us
  Pallas kernels  43.9 us (98%)
  local copies, waits for them, and re-layouts  0.65 us (1%)
    pallas_call x1, Pallas kernels, body(): pl.pallas_call(kernel, out_shape=pltpu.VMEM((tok, half), BF16), in_specs=...  43.9 us

profile of v13, /device:TPU:0, one launch (start us, length us, event | category | flops | bytes accessed | tf_op | source)
XLA Modules:
  0.0 44.6 jit_solution(8092661328536682497)
XLA Ops:
  0.0 43.9 %shard_map.46 = bf16[24,2560]{1,0:T(8,128)(2,1)S(1)} custom-call(bf16[24,2560]{1,0:T(8,128)(2,1)} %x_hbm.1, f32[2560]{0:T(1024)} %gain_hbm.1, bf16[1280,10240]{1,0:T(8,128)(2,1)} %w_in_hbm.1, bf16[5120,2560]{1,0:T(8,128)(2,1)} %w_out_hbm.1), custom_call_target="tpu_custom_call" | custom-call | tf_op jit(solution)/shard_map/pallas_call | solution.py:603
  43.9 0.7 %copy.6 = bf16[24,2560]{1,0:T(8,128)(2,1)} copy(bf16[24,2560]{1,0:T(8,128)(2,1)S(1)} %shard_map.46) | data formatting | bytes 245760

commit v14 on v13

--- a/solution.py
+++ b/solution.py
@@ -196,7 +196,7 @@
         return remote(part_of(d_send, p, part), part_of(d_recv, p, part), d_ssem, d_rsem.at[seq % RING], sibling)
 
     def b_index(j, part):
-        return 9 + j // 2 if part == 2 else j + 5
+        return 9 + j // 2 if part == 2 else j + 4
 
     def x_group(j, part, first, sem):
         return remote(part_of(own, first + j, part), part_of(x_recv, j, part), x_ssem, x_rsem.at[sem], x_next)
@@ -209,24 +209,24 @@
         return c_part(j, WHOLE)
 
     def c_part(j, part):
-        return remote(part_of(own, c0 + j, part), part_of(c_recv.at[0], j, part), c_ssem, c_rsem.at[j], y_next)
+        return remote(part_of(own, c0 + j, part), part_of(c_recv.at[0], j, part), c_ssem, c_rsem.at[home * NC + (1 - home) * j], y_next)
 
     def c_relay(j, part):
-        sem = c_rsem.at[2 * NC + j // 3] if part > 0 else c_rsem.at[NC + j]
+        sem = c_rsem.at[NC + 1 + j // 3] if part > 0 else c_rsem.at[j]
         return remote(part_of(c_recv.at[0], j, part), part_of(c_recv.at[1], j, part), c_ssem, sem, x_next)
 
     last = NA - 1
 
     def both_home():
-        return remote(part_of(own, a0 + last, 1), part_of(c_recv.at[0], NC, 1), c_ssem, c_rsem.at[2 * NC + 2], y_next)
+        return remote(part_of(own, a0 + last, 1), part_of(c_recv.at[0], NC, 1), c_ssem, c_rsem.at[NC + 3], y_next)
 
     def both_far():
-        return remote(part_of(own, a0 + last, 1), part_of(c_recv.at[1], NC, 1), c_ssem, c_rsem.at[2 * NC + 3],
+        return remote(part_of(own, a0 + last, 1), part_of(c_recv.at[1], NC, 1), c_ssem, c_rsem.at[NC + 4],
                       (dp, 1 - y, 2 * (1 - x) + k))
 
     def pass_c(j):
         with jax.named_scope('c_wait'):
-            c_copy(j).wait_recv()
+            remote(c_recv.at[0, j], c_recv.at[0, j], c_ssem, c_rsem.at[j], y_next).wait_recv()
         c_relay(j, FIRST).start()
 
     def up(p, part, seq):
@@ -359,10 +359,11 @@
         if send:
             y_copy(j, part).start()
 
-    def make_h_c(j, part):
+    def make_h_c(j, part, first=False):
         with jax.named_scope('c_wait'):
-            if part == FIRST:
-                c_copy(j).wait_recv()
+            if first:
+                own_part = c_recv.at[0, pl.ds(0, NC)]
+                remote(own_part, own_part, c_ssem, c_rsem.at[NC], y_next).wait_recv()
             c_relay(j, part).wait_recv()
         put_h(c0 + j, part, lambda c: c_recv.at[0, j + c], lambda c: c_recv.at[1, j + c])
         yc_copy(j, part).start()
@@ -385,7 +386,7 @@
 
     def e_copy(group, s):
         r = 2 * (s * x + (1 - s) * (1 - x)) + 1 - k
-        return remote(acc.at[token_rows(group, r)], e_recv[group].at[s], e_ssem, e_rsem.at[2 * group + s], sibling)
+        return remote(acc.at[token_rows(group, r)], e_recv[group].at[s], e_ssem, e_rsem.at[group], sibling)
 
     def f_copy(group):
         return remote(f_send[group], f_recv[group], f_ssem, f_rsem.at[group], x_next)
@@ -396,7 +397,7 @@
 
     def end_send(group):
         with jax.named_scope('e0_wait'):
-            e_copy(group, 0).wait_recv()
+            remote(e_recv[group], e_recv[group], e_ssem, e_rsem.at[group], sibling).wait_recv()
         f_send[group][...] = acc[token_rows(group, 2 * (1 - x) + k), :] + e_recv[group][0]
         f_copy(group).start()
 
@@ -406,8 +407,6 @@
             end_send(0)
 
     def end_sum(group):
-        with jax.named_scope('e1_wait'):
-            e_copy(group, 1).wait_recv()
         with jax.named_scope('f_wait'):
             f_copy(group).wait_recv()
         total = acc[token_rows(group, row), :] + e_recv[group][1] + f_recv[group][...]
@@ -518,13 +517,13 @@
             b_pass(i, part)
             down(2 * NA + i, i, part)
 
-        def c_step(i, part):
-            make_h_c(i, part)
+        def c_step(i, part, first=False):
+            make_h_c(i, part, first)
             down(c0 + i, c0 + i, part)
 
         loop(0, NB, lambda j: make_h(j, FIRST, 0))
         loop(0, NB // 2, lambda m: make_h(2 * m, 2, 0))
-        c_step(0, FIRST)
+        c_step(0, FIRST, first=True)
 
         def step(t):
             c_step(1 + t, FIRST)
@@ -633,11 +632,11 @@
                 dma((N // GROUP,)),
                 dma((2,)),
                 dma((RING,)),
-                dma((NA + 5,)),
-                dma((NA + 5,)),
+                dma((NA + 4,)),
+                dma((NA + 4,)),
                 dma((NB + NB // 2,)),
-                dma((2 * NC + 4,)),
-                dma((4,)),
+                dma((NC + 5,)),
+                dma((2,)),
                 dma((2,)),
             ],
             compiler_params=pltpu.CompilerParams(

time: 44.7 us -> 44.5 us (level)
  no operation moved by 1% of the time
where the time goes in v14:
time: 44.5 us; the launch traced here: 44.4 us
  Pallas kernels  43.7 us (98%)
  local copies, waits for them, and re-layouts  0.65 us (1%)
    pallas_call x1, Pallas kernels, body(): pl.pallas_call(kernel, out_shape=pltpu.VMEM((tok, half), BF16), in_specs=...  43.7 us

profile of v14, /device:TPU:0, one launch (start us, length us, event | category | flops | bytes accessed | tf_op | source)
XLA Modules:
  0.0 44.4 jit_solution(15345044382920938852)
XLA Ops:
  0.0 43.7 %shard_map.46 = bf16[24,2560]{1,0:T(8,128)(2,1)S(1)} custom-call(bf16[24,2560]{1,0:T(8,128)(2,1)} %x_hbm.1, f32[2560]{0:T(1024)} %gain_hbm.1, bf16[1280,10240]{1,0:T(8,128)(2,1)} %w_in_hbm.1, bf16[5120,2560]{1,0:T(8,128)(2,1)} %w_out_hbm.1), custom_call_target="tpu_custom_call" | custom-call | tf_op jit(solution)/shard_map/pallas_call | solution.py:602
  43.7 0.7 %copy.6 = bf16[24,2560]{1,0:T(8,128)(2,1)} copy(bf16[24,2560]{1,0:T(8,128)(2,1)S(1)} %shard_map.46) | data formatting | bytes 245760

commit v15 on v14

--- a/solution.py
+++ b/solution.py
@@ -196,7 +196,7 @@
         return remote(part_of(d_send, p, part), part_of(d_recv, p, part), d_ssem, d_rsem.at[seq % RING], sibling)
 
     def b_index(j, part):
-        return 9 + j // 2 if part == 2 else j + 4
+        return 9 + j // 2 if part == 2 else j + 5
 
     def x_group(j, part, first, sem):
         return remote(part_of(own, first + j, part), part_of(x_recv, j, part), x_ssem, x_rsem.at[sem], x_next)
@@ -326,7 +326,8 @@
     def _():
         x_copy_of(NF, 2, a0).start()
         x_copy_of(NF + 2, 2, a0).start()
-        x_copy_of(NF + 4, 2, a0).start()
+        x_copy_of(NF + 4, 1, a0).start()
+        x_copy_of(NF + 5, 1, a0).start()
         both_far().start()
         x_copy_of(last, 1, a0).start()
 
@@ -491,7 +492,8 @@
         b_step(2, FIRST)
         b_step(NB - 1, FIRST)
         end_start(0)
-        make_h(NF + 4, 2, a0)
+        make_h(NF + 4, 1, a0)
+        make_h(NF + 5, 1, a0)
         end_send_from(0)
         down(NF + 4, a0 + NF + 4, 2)
         c_step(0, 3)
@@ -553,7 +555,10 @@
         put_h(c0 + NC, 1, lambda c: c_recv.at[0, NC + c], lambda c: c_recv.at[1, NC + c])
         down(c0 + NC, a0 + last, 1)
         a_step(NF + 2, 2)
-        a_step(NF + 4, 2)
+        with jax.named_scope('a_wait'):
+            y_copy(NF + 4, 1).wait_recv()
+            y_copy(NF + 5, 1).wait_recv()
+        down(NA + NF + 4, a0 + NF + 4, 2)
 
     end_start(1)
     end_send(1)
@@ -632,8 +637,8 @@
                 dma((N // GROUP,)),
                 dma((2,)),
                 dma((RING,)),
-                dma((NA + 4,)),
-                dma((NA + 4,)),
+                dma((NA + 5,)),
+                dma((NA + 5,)),
                 dma((NB + NB // 2,)),
                 dma((NC + 5,)),
                 dma((2,)),

time: 44.5 us -> 44.4 us (level)
  no operation moved by 1% of the time
where the time goes in v15:
time: 44.4 us; the launch traced here: 44.3 us
  Pallas kernels  43.6 us (98%)
  local copies, waits for them, and re-layouts  0.65 us (1%)
    pallas_call x1, Pallas kernels, body(): pl.pallas_call(kernel, out_shape=pltpu.VMEM((tok, half), BF16), in_specs=...  43.6 us

profile of v15, /device:TPU:0, one launch (start us, length us, event | category | flops | bytes accessed | tf_op | source)
XLA Modules:
  0.0 44.3 jit_solution(8706162318437237202)
XLA Ops:
  0.0 43.6 %shard_map.46 = bf16[24,2560]{1,0:T(8,128)(2,1)S(1)} custom-call(bf16[24,2560]{1,0:T(8,128)(2,1)} %x_hbm.1, f32[2560]{0:T(1024)} %gain_hbm.1, bf16[1280,10240]{1,0:T(8,128)(2,1)} %w_in_hbm.1, bf16[5120,2560]{1,0:T(8,128)(2,1)} %w_out_hbm.1), custom_call_target="tpu_custom_call" | custom-call | tf_op jit(solution)/shard_map/pallas_call | solution.py:607
  43.6 0.7 %copy.6 = bf16[24,2560]{1,0:T(8,128)(2,1)} copy(bf16[24,2560]{1,0:T(8,128)(2,1)S(1)} %shard_map.46) | data formatting | bytes 245760

commit v16 on v15

--- a/solution.py
+++ b/solution.py
@@ -196,7 +196,7 @@
         return remote(part_of(d_send, p, part), part_of(d_recv, p, part), d_ssem, d_rsem.at[seq % RING], sibling)
 
     def b_index(j, part):
-        return 9 + j // 2 if part == 2 else j + 5
+        return 9 + j // 2 if part == 2 else j + 6
 
     def x_group(j, part, first, sem):
         return remote(part_of(own, first + j, part), part_of(x_recv, j, part), x_ssem, x_rsem.at[sem], x_next)
@@ -325,7 +325,8 @@
     @pl.when(home == 0)
     def _():
         x_copy_of(NF, 2, a0).start()
-        x_copy_of(NF + 2, 2, a0).start()
+        x_copy_of(NF + 2, 1, a0).start()
+        x_copy_of(NF + 3, 1, a0).start()
         x_copy_of(NF + 4, 1, a0).start()
         x_copy_of(NF + 5, 1, a0).start()
         both_far().start()
@@ -488,7 +489,9 @@
         loop(3, 5, lambda i: c_step(i, FIRST))
         a_step(NF, 2)
         loop(0, 2, lambda i: b_step(i, FIRST))
-        a_step(NF + 2, 2)
+        make_h(NF + 2, 1, a0)
+        make_h(NF + 3, 1, a0)
+        down(NF + 2, a0 + NF + 2, 2)
         b_step(2, FIRST)
         b_step(NB - 1, FIRST)
         end_start(0)
@@ -554,7 +557,10 @@
             both_far().wait_recv()
         put_h(c0 + NC, 1, lambda c: c_recv.at[0, NC + c], lambda c: c_recv.at[1, NC + c])
         down(c0 + NC, a0 + last, 1)
-        a_step(NF + 2, 2)
+        with jax.named_scope('a_wait'):
+            y_copy(NF + 2, 1).wait_recv()
+            y_copy(NF + 3, 1).wait_recv()
+        down(NA + NF + 2, a0 + NF + 2, 2)
         with jax.named_scope('a_wait'):
             y_copy(NF + 4, 1).wait_recv()
             y_copy(NF + 5, 1).wait_recv()
@@ -637,8 +643,8 @@
                 dma((N // GROUP,)),
                 dma((2,)),
                 dma((RING,)),
-                dma((NA + 5,)),
-                dma((NA + 5,)),
+                dma((NA + 6,)),
+                dma((NA + 6,)),
                 dma((NB + NB // 2,)),
                 dma((NC + 5,)),
                 dma((2,)),

time: 44.4 us -> 44.3 us (level)
  no operation moved by 1% of the time
where the time goes in v16:
time: 44.3 us; the launch traced here: 44.2 us
  Pallas kernels  43.6 us (98%)
  local copies, waits for them, and re-layouts  0.65 us (1%)
    pallas_call x1, Pallas kernels, body(): pl.pallas_call(kernel, out_shape=pltpu.VMEM((tok, half), BF16), in_specs=...  43.6 us

profile of v16, /device:TPU:0, one launch (start us, length us, event | category | flops | bytes accessed | tf_op | source)
XLA Modules:
  0.0 44.2 jit_solution(5307026420249553972)
XLA Ops:
  0.0 43.6 %shard_map.46 = bf16[24,2560]{1,0:T(8,128)(2,1)S(1)} custom-call(bf16[24,2560]{1,0:T(8,128)(2,1)} %x_hbm.1, f32[2560]{0:T(1024)} %gain_hbm.1, bf16[1280,10240]{1,0:T(8,128)(2,1)} %w_in_hbm.1, bf16[5120,2560]{1,0:T(8,128)(2,1)} %w_out_hbm.1), custom_call_target="tpu_custom_call" | custom-call | tf_op jit(solution)/shard_map/pallas_call | solution.py:613
  43.6 0.7 %copy.6 = bf16[24,2560]{1,0:T(8,128)(2,1)} copy(bf16[24,2560]{1,0:T(8,128)(2,1)S(1)} %shard_map.46) | data formatting | bytes 245760
